TPU v7x, 128 devices: a whole 4x4x4 slice. The times are simulated.
128 devices in a mesh: pp: 2 (over core), dp: 64 (over z, y, x).
Axes of the slice: x: 4, y: 4, z: 4, core: 2. Of those that a mesh axis runs over, the one named last changes fastest.
Arguments:
- act_in: bfloat16 [8, 64, 384, 512], P(None, 'dp')
- loss_seed: bfloat16 [8, 64, 384, 512], P(None, 'dp')
- w_qkv: bfloat16 [2, 512, 24, 64], P('pp', 'dp')
- w_proj: bfloat16 [2, 512, 512], P('pp', 'dp')
- w_up: bfloat16 [2, 512, 2048], P('pp', 'dp')
- w_down: bfloat16 [2, 2048, 512], P('pp', 'dp')
Outputs:
- output 1: float32 [2, 512, 24, 64], P('pp', 'dp')
- output 2: float32 [2, 512, 512], P('pp', 'dp')
- output 3: float32 [2, 512, 2048], P('pp', 'dp')
- output 4: float32 [2, 2048, 512], P('pp', 'dp')
- output 5: bfloat16 [8, 64, 384, 512], P(None, 'dp', 'pp')
All inputs are finite; a program needn't handle non-finite values.
Results may differ from a plain program's by a relative error of at most 0.02.
Values are sent between devices in bfloat16 or wider.
A program may use at most 1 GiB of HBM per device.

v0:
```python
import functools

import jax
import jax.numpy as jnp
from jax import lax
from jax.experimental import pallas as pl
from jax.experimental.pallas import tpu as pltpu
from jax.sharding import Mesh
from jax.sharding import PartitionSpec as P

NORM_EPS = 1e-6
BF = jnp.bfloat16
F32 = jnp.float32


def rms_norm(hidden):
    return hidden * lax.rsqrt(jnp.mean(hidden * hidden, axis=-1, keepdims=True) + NORM_EPS)


def dot(a, b):
    return lax.dot_general(a, b, (((1,), (0,)), ((), ())), preferred_element_type=F32)


def dot_nt(a, b):
    return lax.dot_general(a, b, (((1,), (1,)), ((), ())), preferred_element_type=F32)


def dot_tn(a, b):
    return lax.dot_general(a, b, (((0,), (0,)), ((), ())), preferred_element_type=F32)


LOG2E = 1.4426950408889634
GELU_A = 0.7978845608028654
GELU_B = GELU_A * 0.044715


def split_heads(refs, count):
    low = lax.broadcasted_iota(jnp.int32, (refs[0].shape[0], 128), 1) < 64
    zero = jnp.zeros((refs[0].shape[0], 128), BF)
    heads = []
    for h in range(count):
        keep = low if h % 2 == 0 else jnp.logical_not(low)
        lanes = slice((h // 2) * 128, (h // 2) * 128 + 128)
        heads.append([(r[:, lanes], jnp.where(keep, r[:, lanes], zero)) for r in refs])
    return heads


def causal_mask(n):
    return lax.broadcasted_iota(jnp.int32, (n, n), 0) >= lax.broadcasted_iota(jnp.int32, (n, n), 1)


def softmax_rows(s, keep, scale):
    s = jnp.where(keep, s, -1e30)
    e = jnp.exp2((s - jnp.max(s, axis=-1, keepdims=True)) * (scale * LOG2E))
    return e * (1.0 / jnp.sum(e, axis=-1, keepdims=True))


def row_blocks(seq, parts):
    return parts if seq == parts[-1][1] else ((0, seq),)


def attn_fwd_kernel(scale, q_ref, k_ref, v_ref, o_ref):
    seq, lanes = q_ref.shape
    count = lanes // 64
    blocks = row_blocks(seq, ((0, 128), (128, 256), (256, 384)))
    keep = causal_mask(seq)
    heads = split_heads((q_ref, k_ref, v_ref), count)
    scores = [[dot_nt(q[0][a:b], k[1][:b]) for a, b in blocks] for q, k, v in heads]
    probs = [[softmax_rows(s, keep[a:b, :b], scale).astype(BF) for (a, b), s in zip(blocks, row)] for row in scores]
    for h in range(0, count, 2):
        for n, (a, b) in enumerate(blocks):
            pair = dot(probs[h][n], heads[h][2][1][:b]) + dot(probs[h + 1][n], heads[h + 1][2][1][:b])
            o_ref[a:b, (h // 2) * 128:(h // 2) * 128 + 128] = pair.astype(BF)


def attn_bwd_kernel(scale, width, q_ref, k_ref, v_ref, do_ref, dqkv_ref):
    seq, lanes = q_ref.shape
    count = lanes // 64
    blocks = row_blocks(seq, ((0, 256), (256, 384)))
    keep = causal_mask(seq)
    base = pl.program_id(1) * lanes
    heads = split_heads((q_ref, k_ref, v_ref, do_ref), count)
    firsts = [[(dot_nt(q[0][a:b], k[1][:b]), dot_nt(do[0][a:b], v[1][:b])) for a, b in blocks] for q, k, v, do in heads]
    work = []
    for row in firsts:
        done = []
        for (a, b), (s, dp) in zip(blocks, row):
            p = softmax_rows(s, keep[a:b, :b], scale)
            dp = dp.astype(BF).astype(F32)
            delta = jnp.sum(dp * p, axis=-1, keepdims=True)
            done.append((p.astype(BF), (p * (dp - delta) * scale).astype(BF)))
        work.append(done)
    total = lambda terms: functools.reduce(lambda x, y: x + y, terms)
    for j in range(count // 2):
        pair = (2 * j, 2 * j + 1)
        cols = [pl.ds(pl.multiple_of(base + j * 128 + i * width, 128), 128) for i in range(3)]
        for n, (a, b) in enumerate(blocks):
            dqkv_ref[a:b, cols[0]] = total([dot(work[h][n][1], heads[h][1][1][:b]) for h in pair]).astype(BF)
        for i, (_, hi) in enumerate(blocks):
            lo = blocks[i - 1][1] if i else 0
            later = [(n, a, b, h) for n, (a, b) in enumerate(blocks) if n >= i for h in pair]
            dqkv_ref[lo:hi, cols[1]] = total([dot_tn(work[h][n][1][:, lo:hi], heads[h][0][1][a:b]) for n, a, b, h in later]).astype(BF)
            dqkv_ref[lo:hi, cols[2]] = total([dot_tn(work[h][n][0][:, lo:hi], heads[h][3][1][a:b]) for n, a, b, h in later]).astype(BF)


def attn_fwd(qkv, seq, scale):
    tokens, width = qkv.shape[0], qkv.shape[1] // 3
    spec = lambda off: pl.BlockSpec((seq, width), lambda b: (b, off))
    return pl.pallas_call(
        functools.partial(attn_fwd_kernel, scale),
        grid=(tokens // seq,),
        in_specs=[spec(0), spec(1), spec(2)],
        out_specs=spec(0),
        out_shape=jax.ShapeDtypeStruct((tokens, width), BF),
        name="attn_fwd",
    )(qkv, qkv, qkv)


def pre_kernel(h_ref, w_ref, n_ref, qkv_ref):
    normed = rms_norm(h_ref[...].astype(F32)).astype(BF)
    n_ref[...] = normed
    qkv_ref[...] = dot(normed, w_ref[...]).astype(BF)


def whole(shape, layer=None):
    block = shape if layer is None else (None,) + shape
    index = (0,) * len(shape) if layer is None else (layer,) + (0,) * len(shape)
    return pl.BlockSpec(block, lambda *_: index, pipeline_mode=pl.Buffered(1))


def pre_attn(hidden, w_qkv, layer, tile):
    tokens, d = hidden.shape
    cols = w_qkv.shape[2]
    row = lambda n: pl.BlockSpec((tile, n), lambda i: (i, 0))
    return pl.pallas_call(
        pre_kernel,
        grid=(tokens // tile,),
        in_specs=[row(d), whole((d, cols), layer)],
        out_specs=[row(d), row(cols)],
        out_shape=[jax.ShapeDtypeStruct((tokens, d), BF), jax.ShapeDtypeStruct((tokens, cols), BF)],
        name="pre_attn",
    )(hidden, w_qkv)


def post_kernel(h_ref, a_ref, wp_ref, wu_ref, wd_ref, mid_ref, n2_ref, up_ref, ge_ref, out_ref):
    mid = (h_ref[...].astype(F32) + dot(a_ref[...], wp_ref[...])).astype(BF)
    mid_ref[...] = mid
    mid_f32 = mid.astype(F32)
    n2 = rms_norm(mid_f32).astype(BF)
    n2_ref[...] = n2
    ff = wu_ref.shape[1]
    for c in range(0, ff, 512):
        up = dot(n2, wu_ref[:, c:c + 512]).astype(BF)
        up_ref[:, c:c + 512] = up
        u = up.astype(F32)
        t = jnp.tanh(u * (GELU_A + GELU_B * (u * u)))
        ge_ref[:, c:c + 512] = (u * (0.5 * t + 0.5)).astype(BF)
    out_ref[...] = (mid_f32 + dot(ge_ref[...], wd_ref[...])).astype(BF)


def post_attn(hidden, attn, w_proj, w_up, w_down, layer, tile):
    tokens, d = hidden.shape
    ff = w_up.shape[2]
    row = lambda n: pl.BlockSpec((tile, n), lambda i: (i, 0))
    sizes = (d, d, ff, ff, d)
    return pl.pallas_call(
        post_kernel,
        grid=(tokens // tile,),
        in_specs=[row(d), row(d), whole((d, d), layer), whole((d, ff), layer), whole((ff, d), layer)],
        out_specs=[row(n) for n in sizes],
        out_shape=[jax.ShapeDtypeStruct((tokens, n), BF) for n in sizes],
        name="post_attn",
    )(hidden, attn, w_proj, w_up, w_down)


def gelu_pull(u, g):
    u2 = u * u
    s = 0.5 * jnp.tanh(u * (GELU_A + GELU_B * u2)) + 0.5
    return g * (s + (s - s * s) * (u * (2 * GELU_A + (6 * GELU_B) * u2)))


def rms_pull(m, g):
    r = lax.rsqrt(jnp.mean(m * m, axis=-1, keepdims=True) + NORM_EPS)
    return g * r - m * (r * r * r * jnp.mean(g * m, axis=-1, keepdims=True))


MESH = pl.DeviceIdType.MESH
AXES = ("z", "y", "x")
GATHER_ORDER = ((2, 1, 0), (0, 2, 1), (1, 0, 2))
REDUCE_ORDER = ((0, 1, 2), (1, 2, 0), (2, 0, 1))


def step_coord(pos, by):
    return lax.rem(pos + by, 4)


def neighbour(me, axis, by):
    return {AXES[axis]: step_coord(me[axis], by)}


def enter(me, partner):
    barrier = pltpu.get_barrier_semaphore()
    for axis in range(3):
        for by in (1, 3):
            pl.semaphore_signal(barrier, inc=1, device_id=neighbour(me, axis, by), device_id_type=MESH)
    pl.semaphore_signal(barrier, inc=1, device_id={"pp": partner}, device_id_type=MESH)
    pl.semaphore_wait(barrier, 7)


def remote(src, dst, send, recv, where):
    copy = pltpu.make_async_remote_copy(src_ref=src, dst_ref=dst, send_sem=send, recv_sem=recv, device_id=where, device_id_type=MESH)
    copy.start()
    return copy


def gather_kernel(up_ref, down_ref, qkv_ref, proj_ref, wup, wdown, wqkv, wproj, local_sem, send_sem, recv_sem, psend_sem, precv_sem):
    pp = lax.axis_index("pp")
    partner = 1 - pp
    me = tuple(lax.axis_index(a) for a in AXES)
    arrays = ((0, up_ref, wup), (1, down_ref, wdown), (2, qkv_ref, wqkv), (2, proj_ref, wproj))

    def half_of(ref, half):
        rows, cols = ref.shape[-2:]
        lead = (slice(None),) * (len(ref.shape) - 2)
        if rows > 8:
            return ref.at[lead + (pl.ds(half * (rows // 2), rows // 2), slice(None))]
        return ref.at[lead + (slice(None), pl.ds(half * (cols // 2), cols // 2))]

    def block(n, phase, where):
        group, _, out = arrays[n]
        order = GATHER_ORDER[group]
        idx = [None, None, None]
        for later, axis in enumerate(order):
            idx[axis] = slice(None) if later < phase else (where if later == phase else me[axis])
        return out.at[(pp,) + tuple(idx)]

    for n, (_, src, out) in enumerate(arrays):
        pltpu.make_async_copy(src, out.at[(pp,) + me], local_sem.at[n]).start()
    enter(me, partner)
    for n, (_, src, out) in enumerate(arrays):
        pltpu.make_async_copy(src, out.at[(pp,) + me], local_sem.at[n]).wait()

    sends = []
    partners = []

    def tell_partner(ref, n, slot):
        copy = remote(ref, ref, psend_sem.at[n, slot], precv_sem.at[n, slot], {"pp": partner})
        partners.append(copy)

    def send(ref, n, phase, slot, by):
        axis = GATHER_ORDER[arrays[n][0]][phase]
        copy = remote(ref, ref, send_sem.at[n, phase, slot], recv_sem.at[n, phase, slot], neighbour(me, axis, by))
        sends.append(copy)

    def arrived(ref, n, phase, slot):
        pltpu.make_async_copy(ref, ref, recv_sem.at[n, phase, slot]).wait()

    for phase in range(3):
        last = phase == 2
        place = [me[GATHER_ORDER[arrays[n][0]][phase]] for n in range(4)]
        for n in range(4):
            mine = block(n, phase, place[n])
            send(half_of(mine, 0), n, phase, 0, 1)
            send(half_of(mine, 1), n, phase, 1, 3)
        for n in range(4):
            mine = block(n, phase, place[n])
            send(half_of(mine, 1), n, phase, 2, 1)
            send(half_of(mine, 0), n, phase, 3, 3)
            if last:
                tell_partner(mine, n, 0)
        for n in range(4):
            left = block(n, phase, step_coord(place[n], 3))
            right = block(n, phase, step_coord(place[n], 1))
            arrived(half_of(left, 0), n, phase, 0)
            send(half_of(left, 0), n, phase, 4, 1)
            if last:
                tell_partner(half_of(left, 0), n, 1)
            arrived(half_of(right, 1), n, phase, 1)
            send(half_of(right, 1), n, phase, 5, 3)
            if last:
                tell_partner(half_of(right, 1), n, 2)
        for n in range(4):
            left = block(n, phase, step_coord(place[n], 3))
            right = block(n, phase, step_coord(place[n], 1))
            arrived(half_of(left, 1), n, phase, 2)
            if last:
                tell_partner(half_of(left, 1), n, 3)
            arrived(half_of(right, 0), n, phase, 3)
            if last:
                tell_partner(half_of(right, 0), n, 4)
        for n in range(4):
            far = block(n, phase, step_coord(place[n], 2))
            arrived(half_of(far, 0), n, phase, 4)
            if last:
                tell_partner(half_of(far, 0), n, 5)
            arrived(half_of(far, 1), n, phase, 5)
            if last:
                tell_partner(half_of(far, 1), n, 6)
    for copy in sends:
        copy.wait_send()
    for copy in partners:
        copy.wait_send()
    for copy in partners:
        copy.wait_recv()


def gather_weights(w_qkv, w_proj, w_up, w_down):
    vmem = pl.BlockSpec(memory_space=pltpu.VMEM)
    full = lambda w: jax.ShapeDtypeStruct((2, 4, 4, 4) + w.shape, BF)
    dma = pltpu.SemaphoreType.DMA
    args = (w_up, w_down, w_qkv, w_proj)
    outs = pl.pallas_call(
        gather_kernel,
        in_specs=[vmem] * 4,
        out_specs=[vmem] * 4,
        out_shape=[full(w) for w in args],
        scratch_shapes=[dma((4,)), dma((4, 3, 6)), dma((4, 3, 6)), dma((4, 7)), dma((4, 7))],
        compiler_params=pltpu.CompilerParams(collective_id=0, has_side_effects=True, vmem_limit_bytes=40 << 20),
        name="gather_weights",
    )(*args)
    flat = [o.reshape(2, -1, o.shape[-1]) for o in outs]
    return flat[2], flat[3], flat[0], flat[1]


REDUCE_OFFSETS = (2, 1, 3, 0)


def reduce_pieces(refs, color, core):
    up_ref, down_ref, qkv_ref, proj_ref = refs
    if color == 0:
        return [(up_ref, pl.ds(0, 8), pl.ds(pl.multiple_of(core * 1024 + h * 512, 128), 512), h, pl.ds(0, 512)) for h in range(2)]
    if color == 1:
        return [(down_ref, pl.ds(pl.multiple_of(core * 16 + h * 8, 8), 8), pl.ds(0, 512), h, pl.ds(0, 512)) for h in range(2)]
    return [
        (qkv_ref, pl.ds(0, 8), pl.ds(pl.multiple_of(core * 768, 128), 512), 0, pl.ds(0, 512)),
        (qkv_ref, pl.ds(0, 8), pl.ds(pl.multiple_of(core * 768 + 512, 128), 256), 1, pl.ds(0, 256)),
        (proj_ref, pl.ds(0, 8), pl.ds(pl.multiple_of(core * 256, 128), 256), 1, pl.ds(256, 256)),
    ]


def add_block(out, dst, src):
    dims = dst.shape[:-2]
    total = 1
    for s in dims:
        total *= s

    def spread(flat, inner):
        index = []
        for s in reversed(inner):
            index.append(flat % s)
            flat //= s
        return tuple(reversed(index))

    def one(index):
        out[index] = dst[index] + src[index]

    if total <= 4:
        for flat in range(total):
            one(spread(flat, dims))
        return

    def body(i, _):
        for flat in range(total // dims[0]):
            one((i,) + spread(flat, dims[1:]))
        return 0

    lax.fori_loop(0, dims[0], body, 0)


class Reducer:
    def __init__(self, acc, slots, sems, start=0):
        self.pp = lax.axis_index("pp")
        self.partner = 1 - self.pp
        self.me = tuple(lax.axis_index(a) for a in AXES)
        self.acc, self.slots, self.start = acc, slots, start
        self.send_sem, self.recv_sem = sems

    def lead(self, color, phase, where):
        order = REDUCE_ORDER[color]
        idx = [None, None, None]
        for later, axis in enumerate(order):
            idx[axis] = self.me[axis] if later < phase else (where if later == phase else slice(None))
        return tuple(v for axis, v in enumerate(idx) if order.index(axis) >= self.start)

    def place(self, color, phase, by):
        return step_coord(self.me[REDUCE_ORDER[color][phase]], by)

    def loads(self, refs, sem, color, pos):
        where = self.lead(color, 0, self.place(color, 0, REDUCE_OFFSETS[pos]))
        return [
            pltpu.make_async_copy(ref.at[where + (rows, cols)], self.acc.at[(color,) + where + (h, slice(None), into)], sem.at[color, pos, n])
            for n, (ref, rows, cols, h, into) in enumerate(reduce_pieces(refs, color, self.pp))
        ]

    def swaps(self, refs, peer, sems, color, pos):
        where = self.lead(color, 0, self.place(color, 0, REDUCE_OFFSETS[pos]))
        return [
            pltpu.make_async_remote_copy(
                src_ref=ref.at[where + (rows, cols)], dst_ref=peer.at[(color,) + where + (h, slice(None), into)],
                send_sem=sems[0].at[color, pos, n], recv_sem=sems[1].at[color, pos, n], device_id={"pp": self.partner}, device_id_type=MESH)
            for n, (ref, rows, cols, h, into) in enumerate(reduce_pieces(refs, color, self.partner))
        ]

    def part(self, color, phase, by, half):
        return self.acc.at[(color,) + self.lead(color, phase, self.place(color, phase, by)) + (half,)]

    def near(self, color, phase, side):
        return self.slots[phase][0].at[color, side]

    def final(self, color, phase, side, half):
        return self.slots[phase][1].at[color, side, half]

    def copy(self, color, phase, n):
        part, near, final = self.part, self.near, self.final
        plan = (
            (part(color, phase, 2, 0), near(color, phase, 0), 1),
            (part(color, phase, 2, 1), near(color, phase, 1), 3),
            (part(color, phase, 1, 1), final(color, phase, 0, 1), 1),
            (part(color, phase, 3, 0), final(color, phase, 1, 0), 3),
            (part(color, phase, 1, 0), final(color, phase, 0, 0), 1),
            (part(color, phase, 3, 1), final(color, phase, 1, 1), 3),
        )
        k = phase - self.start
        src, dst, by = plan[n]
        return pltpu.make_async_remote_copy(
            src_ref=src, dst_ref=dst, send_sem=self.send_sem.at[color, k, n], recv_sem=self.recv_sem.at[color, k, n],
            device_id=neighbour(self.me, REDUCE_ORDER[color][phase], by), device_id_type=MESH)

    def first_sends(self, color, phase, by):
        for n in {2: (0, 1), 1: (2,), 3: (3,), 0: ()}[by]:
            self.copy(color, phase, n).start()

    def swapped(self, refs, peer, load_sem, swap_sems, pos):
        by = REDUCE_OFFSETS[pos]
        for color in range(3):
            for copy in self.loads(refs, load_sem, color, pos):
                copy.wait()
            for copy in self.swaps(refs, peer, swap_sems, color, pos):
                copy.wait_recv()
            block = self.acc.at[(color,) + self.lead(color, 0, self.place(color, 0, by))]
            add_block(block, block, peer.at[(color,) + self.lead(color, 0, self.place(color, 0, by))])
            self.first_sends(color, 0, by)

    def all_first(self, phase):
        for by in (2, 1, 3):
            for color in range(3):
                self.first_sends(color, phase, by)

    def second(self, phase):
        for color in range(3):
            for n, by, half in ((0, 1, 0), (1, 3, 1)):
                self.copy(color, phase, n).wait_recv()
                dst = self.part(color, phase, by, half)
                add_block(dst, dst, self.near(color, phase, n))
                self.copy(color, phase, n + 4).start()

    def third(self, phase):
        for color in range(3):
            for n, side, half in ((2, 0, 1), (3, 1, 0)):
                self.copy(color, phase, n).wait_recv()
                dst = self.part(color, phase, 0, half)
                add_block(dst, dst, self.final(color, phase, side, half))

    def fourth(self, phase, out=None):
        for color in range(3):
            for n, side, half in ((4, 0, 0), (5, 1, 1)):
                self.copy(color, phase, n).wait_recv()
                dst = self.part(color, phase, 0, half)
                add_block(dst if out is None else out.at[color, :, :, half], dst, self.final(color, phase, side, half))

    def drain(self, phase):
        for color in range(3):
            for n in range(6):
                self.copy(color, phase, n).wait_send()

    def finals(self, outs, sems):
        copies = []
        for color in range(3):
            for n, (out, rows, cols, h, into) in enumerate(reduce_pieces(outs, color, self.pp)):
                where = self.lead(color, 3, None)
                copies.append((out.at[rows, cols], self.acc.at[(color,) + where + (h, slice(None), into)], pltpu.make_async_remote_copy(
                    src_ref=self.acc.at[(color,) + where + (h, slice(None), into)], dst_ref=out.at[rows, cols],
                    send_sem=sems[0].at[color, n], recv_sem=sems[1].at[color, n], device_id={"pp": self.partner}, device_id_type=MESH)))
        return copies


def give_finals(red, outs, sems):
    for dst, src, copy in red.finals(outs, sems):
        copy.start()
        dst[...] = src[...]


def end_finals(red, outs, sems):
    for _, _, copy in red.finals(outs, sems):
        copy.wait_send()
        copy.wait_recv()


def reduce_kernel(up_ref, down_ref, qkv_ref, proj_ref, oup, odown, oqkv, oproj,
                  acc, peer, t1a, t2a, t1b, t2b, t1c, t2c,
                  load_sem, psend_sem, precv_sem, send_sem, recv_sem, fsend_sem, frecv_sem):
    refs, outs = (up_ref, down_ref, qkv_ref, proj_ref), (oup, odown, oqkv, oproj)
    red = Reducer(acc, ((t1a, t2a), (t1b, t2b), (t1c, t2c)), (send_sem, recv_sem))
    swap_sems, final_sems = (psend_sem, precv_sem), (fsend_sem, frecv_sem)
    for pos in range(4):
        for color in range(3):
            for copy in red.loads(refs, load_sem, color, pos):
                copy.start()
    enter(red.me, red.partner)
    for pos in range(4):
        for color in range(3):
            for copy in red.swaps(refs, peer, swap_sems, color, pos):
                copy.start()
    for pos in range(4):
        red.swapped(refs, peer, load_sem, swap_sems, pos)
    for phase in range(3):
        if phase:
            red.all_first(phase)
        red.second(phase)
        red.third(phase)
        red.fourth(phase)
    give_finals(red, outs, final_sems)
    end_finals(red, outs, final_sems)
    for phase in range(3):
        red.drain(phase)
    for pos in range(4):
        for color in range(3):
            for copy in red.swaps(refs, peer, swap_sems, color, pos):
                copy.wait_send()


def grad_views(grads):
    g_qkv, g_proj, g_up, g_down = grads
    return [g.reshape(4, 4, 4, g.shape[0] // 64, g.shape[1]) for g in (g_up, g_down, g_qkv, g_proj)]


VMEM, DMA = pltpu.VMEM, pltpu.SemaphoreType.DMA
SWAP_SCRATCH = [VMEM((3, 4, 4, 4, 2, 8, 512), F32), VMEM((3, 4, 4, 4, 2, 8, 512), F32)]
PHASE_SCRATCH = [
    [VMEM((3, 2, 4, 4, 8, 512), F32), VMEM((3, 2, 2, 4, 4, 8, 512), F32)],
    [VMEM((3, 2, 4, 8, 512), F32), VMEM((3, 2, 2, 4, 8, 512), F32)],
    [VMEM((3, 2, 8, 512), F32), VMEM((3, 2, 2, 8, 512), F32)],
]
SWAP_SEMS = [DMA((3, 4, 3)), DMA((3, 4, 3)), DMA((3, 4, 3))]
PHASE_SEMS = lambda n: [DMA((3, n, 6)), DMA((3, n, 6))]
FINAL_SEMS = [DMA((3, 3)), DMA((3, 3))]


def reduce_grads(grads, which):
    args = grad_views(grads)
    outs = pl.pallas_call(
        reduce_kernel,
        in_specs=[pl.BlockSpec(memory_space=pl.ANY)] * 4,
        out_specs=[pl.BlockSpec(memory_space=VMEM)] * 4,
        out_shape=[jax.ShapeDtypeStruct(a.shape[3:], F32) for a in args],
        scratch_shapes=SWAP_SCRATCH + sum(PHASE_SCRATCH, []) + SWAP_SEMS + PHASE_SEMS(3) + FINAL_SEMS,
        compiler_params=pltpu.CompilerParams(collective_id=1 + which, has_side_effects=True, vmem_limit_bytes=30 << 20),
        name="reduce_grads",
    )(*args)
    return outs[2], outs[3], outs[0], outs[1]


def ffn_bwd_kernel(tile, carry, *refs):
    ge_ref, up_ref, ct_ref, n2_ref, mid_ref, at_ref, wd_ref, wu_ref, wp_ref = refs[:9]
    refs = refs[9:]
    step = pl.program_id(0)
    last = pl.num_programs(0) - 1
    at = lambda k, f: pl.when(step == k)(f)
    if carry:
        grads, refs = refs[:4], refs[4:]
        reduced = refs[5]
        acc_g, peer, near, final, load_sem, psend, precv, send_sem, recv_sem = refs[8:]
        red = Reducer(acc_g, ((near, final),), (send_sem, recv_sem))
        swap_sems = (psend, precv)
    gd_ref, gu_ref, gp_ref, cm_ref, ca_ref = refs[:5]
    acc, ctu = refs[6:8] if carry else refs[5:7]

    def every(what):
        for pos in range(4):
            for color in range(3):
                for copy in what(color, pos):
                    yield copy

    def begin():
        for copy in every(lambda color, pos: red.loads(grads, load_sem, color, pos)):
            copy.start()
        enter(red.me, red.partner)
        for copy in every(lambda color, pos: red.swaps(grads, peer, swap_sems, color, pos)):
            copy.start()

    def finish():
        red.fourth(0, reduced)
        red.drain(0)
        for copy in every(lambda color, pos: red.swaps(grads, peer, swap_sems, color, pos)):
            copy.wait_send()

    def swapped(*positions):
        for pos in positions:
            red.swapped(grads, peer, load_sem, swap_sems, pos)

    def carried_step():
        if carry:
            todo = {
                0: begin,
                1: lambda: swapped(0, 1, 2, 3),
                2: lambda: red.second(0),
                3: lambda: red.third(0),
            }
            for k, f in todo.items():
                at(k, f)

    carried_step()
    chunks = range(0, ct_ref.shape[0], tile)
    for m in chunks:
        rows = slice(m, m + tile)
        cg = dot_nt(ct_ref[rows, :], wd_ref[...]).astype(BF).astype(F32)
        ctu[rows, :] = gelu_pull(up_ref[rows, :].astype(F32), cg).astype(BF)
    gd_ref[...] = dot_tn(ge_ref[...], ct_ref[...])
    gu_ref[...] = dot_tn(n2_ref[...], ctu[...])
    part = dot_nt(ctu[...], wu_ref[...])

    @pl.when(step == 0)
    def _():
        acc[...] = part

    @pl.when(step > 0)
    def _():
        acc[...] += part

    @pl.when(step == last)
    def _():
        pulled = rms_pull(mid_ref[...].astype(F32), acc[...].astype(BF).astype(F32))
        cm_ref[...] = (ct_ref[...].astype(F32) + pulled).astype(BF)
        ca_ref[...] = dot_nt(cm_ref[...], wp_ref[...]).astype(BF)
        gp_ref[...] = dot_tn(at_ref[...], cm_ref[...])

    if carry:
        at(last, finish)


def ffn_bwd(gelu, up, ct, normed2, mid, attn, w_down, w_up, w_proj, layer, tile, carried):
    tokens, d = ct.shape
    ff = gelu.shape[1]
    part = 512
    act = whole((tokens, d))
    cols = pl.BlockSpec((tokens, part), lambda i: (0, i))
    in_specs = [cols, cols, act, act, act, act,
                pl.BlockSpec((None, part, d), lambda i: (layer, i, 0)), pl.BlockSpec((None, d, part), lambda i: (layer, 0, i)), whole((d, d), layer)]
    out_specs = [pl.BlockSpec((part, d), lambda i: (i, 0)), pl.BlockSpec((d, part), lambda i: (0, i)), whole((d, d)), act, act]
    out_shape = [jax.ShapeDtypeStruct((ff, d), F32), jax.ShapeDtypeStruct((d, ff), F32), jax.ShapeDtypeStruct((d, d), F32),
                 jax.ShapeDtypeStruct((tokens, d), BF), jax.ShapeDtypeStruct((tokens, d), BF)]
    scratch = [VMEM((tokens, d), F32), VMEM((tokens, part), BF)]
    params = dict(vmem_limit_bytes=50 << 20)
    args = (gelu, up, ct, normed2, mid, attn, w_down, w_up, w_proj)
    carry = carried is not None
    if carry:
        args = args + tuple(grad_views(carried))
        in_specs = in_specs + [pl.BlockSpec(memory_space=pl.ANY)] * 4
        out_specs = out_specs + [whole((3, 4, 4, 2, 8, 512))]
        out_shape = out_shape + [jax.ShapeDtypeStruct((3, 4, 4, 2, 8, 512), F32)]
        scratch = scratch + SWAP_SCRATCH + PHASE_SCRATCH[0] + SWAP_SEMS + PHASE_SEMS(1)
        params = dict(vmem_limit_bytes=62 << 20, collective_id=2, has_side_effects=True)
    return pl.pallas_call(
        functools.partial(ffn_bwd_kernel, tile, carry),
        grid=(ff // part,), in_specs=in_specs, out_specs=out_specs, out_shape=out_shape, scratch_shapes=scratch,
        compiler_params=pltpu.CompilerParams(**params),
        name="ffn_bwd_carry" if carry else "ffn_bwd",
    )(*args)


def attn_carry_kernel(scale, width, q_ref, k_ref, v_ref, do_ref, acc_hbm, dqkv_ref, *rest):
    results, (acc_ref, sup, sdown, sqkv, sproj, t1b, t2b, t1c, t2c, load_sem, send_sem, recv_sem, fsend_sem, frecv_sem) = rest[:4], rest[4:]
    steps = pl.num_programs(1)
    step = pl.program_id(0) * steps + pl.program_id(1)
    red = Reducer(acc_ref, (None, (t1b, t2b), (t1c, t2c)), (send_sem, recv_sem), start=1)
    outs, sems = (sup, sdown, sqkv, sproj), (fsend_sem, frecv_sem)

    def begin():
        load = pltpu.make_async_copy(acc_hbm, acc_ref, load_sem)
        load.start()
        enter(red.me, red.partner)
        load.wait()
        red.all_first(1)

    def turn():
        red.fourth(1)
        red.all_first(2)

    def close():
        red.fourth(2)
        give_finals(red, outs, sems)

    def third_second():
        red.third(1)

    todo = {0: begin, 2: lambda: red.second(1), 3: third_second, 4: turn, 5: lambda: red.second(2), 6: lambda: red.third(2), 7: close}
    for k, f in todo.items():
        pl.when(step == k)(f)
    attn_bwd_kernel(scale, width, q_ref, k_ref, v_ref, do_ref, dqkv_ref)

    @pl.when(step == pl.num_programs(0) * steps - 1)
    def _():
        end_finals(red, outs, sems)
        red.drain(1)
        red.drain(2)
        for result, out in zip(results, outs):
            result[...] = out[...]


def attn_bwd(qkv, do, seq, scale, carried):
    tokens, width = qkv.shape[0], qkv.shape[1] // 3
    steps = width // 256
    spec = lambda off: pl.BlockSpec((seq, 256), lambda b, j: (b, off + j))
    in_specs = [spec(0), spec(steps), spec(2 * steps), spec(0)]
    out_specs = [pl.BlockSpec((seq, 3 * width), lambda b, j: (b, 0))]
    out_shape = [jax.ShapeDtypeStruct((tokens, 3 * width), BF)]
    args, scratch, params, kernel = (qkv, qkv, qkv, do), [], {}, attn_bwd_kernel
    if carried is not None:
        args = args + (carried,)
        kernel = attn_carry_kernel
        in_specs = in_specs + [pl.BlockSpec(memory_space=pl.ANY)]
        shapes = ((8, 2048), (32, 512), (8, 1536), (8, 512))
        out_specs = out_specs + [whole(s) for s in shapes]
        out_shape = out_shape + [jax.ShapeDtypeStruct(s, F32) for s in shapes]
        scratch = [VMEM(s, F32) for s in (carried.shape,) + shapes] + PHASE_SCRATCH[1] + PHASE_SCRATCH[2] + [DMA] + PHASE_SEMS(2) + FINAL_SEMS
        params = dict(collective_id=3, has_side_effects=True, vmem_limit_bytes=50 << 20)
    return pl.pallas_call(
        functools.partial(kernel, scale, width),
        grid=(tokens // seq, steps), in_specs=in_specs, out_specs=out_specs, out_shape=out_shape, scratch_shapes=scratch,
        compiler_params=pltpu.CompilerParams(**params),
        name="attn_bwd" if carried is None else "attn_bwd_carry",
    )(*args)


def layer_forward(hidden, weights, layer, seq, scale):
    w_qkv, w_proj, w_up, w_down = weights
    normed, qkv = pre_attn(hidden, w_qkv, layer, seq)
    attn = attn_fwd(qkv, seq, scale)
    mid, normed2, up, gelu, out = post_attn(hidden, attn, w_proj, w_up, w_down, layer, seq)
    return out, (hidden, normed, qkv, attn, mid, normed2, up, gelu)


def layer_backward(saved, ct_out, weights, layer, seq, scale, carried):
    w_qkv, w_proj, w_up, w_down = weights
    hidden, normed, qkv, attn, mid, normed2, up, gelu = saved
    res = ffn_bwd(gelu, up, ct_out, normed2, mid, attn, w_down, w_up, w_proj, layer, seq, carried)
    g_down, g_up, g_proj, ct_mid, ct_attn = res[:5]
    res = attn_bwd(qkv, ct_attn, seq, scale, res[5] if carried is not None else None)
    ct_qkv = res[0]
    g_qkv = dot_tn(normed, ct_qkv)
    grads = (g_qkv, g_proj, g_up, g_down)
    if carried is not None:
        return grads, (res[3], res[4], res[1], res[2])
    ct_norm = dot_nt(ct_qkv, w_qkv[layer]).astype(BF)
    ct_hidden = (ct_mid.astype(F32) + rms_pull(hidden.astype(F32), ct_norm.astype(F32))).astype(BF)
    return grads, ct_hidden


def solution(mesh):
    stages = mesh.shape['pp']
    grid = Mesh(mesh.devices.reshape(2, 4, 4, 4), ("pp", "z", "y", "x"))
    dp = ("z", "y", "x")
    swap = [(0, 1), (1, 0)]

    def device_step(act_in, loss_seed, w_qkv, w_proj, w_up, w_down):
        micro, _, seq, d = act_in.shape
        mine = micro // 2
        pp = lax.axis_index('pp')
        heads3, hd = w_qkv.shape[2:]
        scale = hd ** -0.5

        full = gather_weights(*(w.reshape(w.shape[1], -1) for w in (w_qkv, w_proj, w_up, w_down)))
        act = lax.dynamic_slice_in_dim(act_in, pp * mine, mine, 0).reshape(mine * seq, d)
        seed = lax.dynamic_slice_in_dim(loss_seed, pp * mine, mine, 0).reshape(mine * seq, d)
        h1, saved0 = layer_forward(act, full, 0, seq, scale)
        h2, saved1 = layer_forward(h1, full, 1, seq, scale)

        out4 = h2.reshape(mine, 1, seq, d)
        half = seq // 2
        keep = lax.dynamic_slice_in_dim(out4, pp * half, half, 2)
        give = lax.dynamic_slice_in_dim(out4, (1 - pp) * half, half, 2)
        got = lax.ppermute(give, 'pp', swap)
        act_out = jnp.concatenate([jnp.where(pp == 0, keep, got), jnp.where(pp == 0, got, keep)], axis=0)

        grads1, ct1 = layer_backward(saved1, seed, full, 1, seq, scale, None)
        grads0, red1 = layer_backward(saved0, ct1, full, 0, seq, scale, grads1)
        red0 = reduce_grads(grads0, 0)
        outs = [jnp.where(pp == 0, a, b) for a, b in zip(red0, red1)]
        return tuple(o.reshape(w.shape) for o, w in zip(outs, (w_qkv, w_proj, w_up, w_down))) + (act_out,)

    weight_spec = P('pp', dp)
    act_spec = P(None, dp)
    return jax.shard_map(device_step, mesh=grid, in_specs=(act_spec, act_spec) + (weight_spec,) * 4, out_specs=(weight_spec,) * 4 + (P(None, dp, 'pp'),), check_vma=False)
```

profile of v0, /device:TPU:1, one launch (start us, length us, event | category | flops | bytes accessed | tf_op | source)
XLA Modules:
  0.0 303.8 jit_solution(15367098796302506052)
XLA Ops:
  0.6 0.9 reshape.104.qkv_ref
  1.6 3.8 %constant_dynamic-slice_fusion.1 = (bf16[4,1,384,512]{3,2,1,0:T(8,128)(2,1)}, bf16[4,1,384,512]{3,2,1,0:T(8,128)(2,1)}) fusion(bf16[8,1,384,512]{3,2,1,0:T(8,128)(2,1)} %param.7, s32[]{:T(128)S(6)} %select_n.55, bf16[8,1,384,512]{3,2,1,0:T(8,128)(2,1)} %param.6), kind=kLoop, calls=%fused_computation.21 | loop fusion | bytes 6291460 | tf_op jit(solution)/shard_map/dynamic_slice | solution.py:774
  5.4 43.8 %gather_weights.1 = (bf16[2,4,4,4,8,2048]{5,4,3,2,1,0:T(8,128)(2,1)S(1)}, bf16[2,4,4,4,32,512]{5,4,3,2,1,0:T(8,128)(2,1)S(1)}, bf16[2,4,4,4,8,1536]{5,4,3,2,1,0:...) custom-call(bf16[8,2048]{1,0:T(8,128)(2,1)S(1)} %bitcast.55, bf16[32,512]{1,0:T(8,128)(2,1)S(1)} %bitcast.56, ...), custom_call_target="tpu_custom_call" | custom-call | tf_op jit(solution)/shard_map/gather_weights/pallas_call | solution.py:312
  49.3 2.0 copy-done
  51.2 2.0 copy-done.1
  53.2 1.6 copy-done.2
  54.8 1.0 copy-done.4
  55.8 6.7 %pre_attn.2 = (bf16[1536,512]{1,0:T(8,128)(2,1)}, bf16[1536,1536]{1,0:T(8,128)(2,1)}) custom-call(bf16[1536,512]{1,0:T(8,128)(2,1)} %bitcast.58, bf16[2,512,1536]{2,1,0:T(8,128)(2,1)} %bitcast.44), custom_call_target="tpu_custom_call" | custom-call | tf_op jit(solution)/shard_map/pre_attn/pallas_call | solution.py:135
  62.5 8.7 %attn_fwd.2.a_ref.refs_5_ = bf16[1536,512]{1,0:T(8,128)(2,1)} custom-call(bf16[1536,1536]{1,0:T(8,128)(2,1)} %get-tuple-element.43.q_ref.k_ref.v_ref, bf16[1536,1536]{1,0:T(8,128)(2,1)} %get-tuple-element.43.q_ref.k_ref.v_ref, bf16[1536,1536]{1,0:T(8,128)(2,1)} %get-tuple-element.43.q_ref.k_ref.v_ref), custom_call_target="tpu_custom_call" | custom-call | tf_op jit(solution)/shard_map/attn_fwd/pallas_call | solution.py:109
  71.2 15.7 %post_attn.2 = (bf16[1536,512]{1,0:T(8,128)(2,1)}, bf16[1536,512]{1,0:T(8,128)(2,1)}, bf16[1536,2048]{1,0:T(8,128)(2,1)}, bf16[1536,2048]{1,0:T(8,128)(2,1)}, bf16[1536,512]{1,0:T(8,128)(2,1)}) custom-call(bf16[1536,512]{1,0:T(8,128)(2,1)} %bitcast.59, bf16[1536,512]{1,0:T(8,128)(2,1)} %attn_fwd.2.a_ref.refs_5_, bf16[2,512,512]{2,1,0:T(8,128)(2,1)} %bitcast.46, ...), custom_call_target="tpu_custom_call" | custom-call | tf_op jit(solution)/shard_map/post_attn/pallas_call | solution.py:166
  86.9 6.6 %pre_attn.3 = (bf16[1536,512]{1,0:T(8,128)(2,1)}, bf16[1536,1536]{1,0:T(8,128)(2,1)}) custom-call(bf16[1536,512]{1,0:T(8,128)(2,1)} %get-tuple-element.49.h_ref, bf16[2,512,1536]{2,1,0:T(8,128)(2,1)} %bitcast.45), custom_call_target="tpu_custom_call" | custom-call | tf_op jit(solution)/shard_map/pre_attn/pallas_call | solution.py:135
  93.5 8.7 %attn_fwd.3.a_ref.refs_5_ = bf16[1536,512]{1,0:T(8,128)(2,1)} custom-call(bf16[1536,1536]{1,0:T(8,128)(2,1)} %get-tuple-element.50.q_ref.k_ref.v_ref, bf16[1536,1536]{1,0:T(8,128)(2,1)} %get-tuple-element.50.q_ref.k_ref.v_ref, bf16[1536,1536]{1,0:T(8,128)(2,1)} %get-tuple-element.50.q_ref.k_ref.v_ref), custom_call_target="tpu_custom_call" | custom-call | tf_op jit(solution)/shard_map/attn_fwd/pallas_call | solution.py:109
  102.2 16.0 %post_attn.3 = (bf16[1536,512]{1,0:T(8,128)(2,1)}, bf16[1536,512]{1,0:T(8,128)(2,1)}, bf16[1536,2048]{1,0:T(8,128)(2,1)}, bf16[1536,2048]{1,0:T(8,128)(2,1)}, bf16[1536,512]{1,0:T(8,128)(2,1)}) custom-call(bf16[1536,512]{1,0:T(8,128)(2,1)} %get-tuple-element.49.h_ref, bf16[1536,512]{1,0:T(8,128)(2,1)} %attn_fwd.3.a_ref.refs_5_, ...), custom_call_target="tpu_custom_call" | custom-call | tf_op jit(solution)/shard_map/post_attn/pallas_call | solution.py:166
  118.2 2.1 constant_dynamic-slice_fusion
  120.7 1.3 slice.4
  122.4 24.4 %ffn_bwd.1 = (f32[2048,512]{1,0:T(8,128)}, f32[512,2048]{1,0:T(8,128)}, f32[512,512]{1,0:T(8,128)S(1)}, bf16[1536,512]{1,0:T(8,128)(2,1)S(1)}, bf16[1536,512]{1,0:T(8,128)(2,1)}) custom-call(bf16[1536,2048]{1,0:T(8,128)(2,1)} %get-tuple-element.51.refs_0_, bf16[1536,2048]{1,0:T(8,128)(2,1)} %get-tuple-element.52.refs_1_, bf16[1536,512]{1,0:T(8,128)(2,1)} %bitcast.60, ...), custom_call_target="tpu_custom_call" | custom-call | tf_op jit(solution)/shard_map/ffn_bwd/pallas_call | solution.py:663
  146.8 1.0 copy-done.10
  147.8 19.2 %attn_bwd.1 = bf16[1536,1536]{1,0:T(8,128)(2,1)} custom-call(bf16[1536,1536]{1,0:T(8,128)(2,1)} %get-tuple-element.50.q_ref.k_ref.v_ref, bf16[1536,1536]{1,0:T(8,128)(2,1)} %get-tuple-element.50.q_ref.k_ref.v_ref, bf16[1536,1536]{1,0:T(8,128)(2,1)} %get-tuple-element.50.q_ref.k_ref.v_ref, bf16[1536,512]{1,0:T(8,128)(2,1)} %get-tuple-element.56.do_ref), custom_call_target="tpu_custom_call" | custom-call | tf_op jit(solution)/shard_map/attn_bwd/pallas_call | solution.py:727
  167.0 5.8 %fusion.3 = (f32[1536]{0:T(1024)S(1)}, f32[1536]{0:T(1024)S(1)}, bf16[1536,512]{1,0:T(8,128)(2,1)S(1)}) fusion(bf16[1536,512]{1,0:T(8,128)(2,1)S(1)} %copy-done.15, bf16[1536,1536]{1,0:T(8,128)(2,1)} %attn_bwd.1, bf16[512,1536]{1,0:T(8,128)(2,1)} %bitcast.64), kind=kOutput, calls=%fused_computation.7 | convolution fusion | flops 2421421056 | bytes 9449472 | tf_op jit(solution)/shard_map/dot_general | solution.py:25
  172.9 4.3 %fusion.6 = f32[512,1536]{1,0:T(8,128)} fusion(bf16[1536,512]{1,0:T(8,128)(2,1)S(1)} %copy-done.19, bf16[1536,1536]{1,0:T(8,128)(2,1)S(1)} %copy-done.16), kind=kOutput, calls=%fused_computation.23 | convolution fusion | flops 2415919104 | bytes 9437184 | tf_op jit(solution)/shard_map/dot_general | solution.py:29
  177.1 1.9 fusion.2.refs_2_
  179.1 45.1 %ffn_bwd_carry.1 = (f32[2048,512]{1,0:T(8,128)}, f32[512,2048]{1,0:T(8,128)}, f32[512,512]{1,0:T(8,128)}, bf16[1536,512]{1,0:T(8,128)(2,1)}, bf16[1536,512]{1,0:...) custom-call(bf16[1536,2048]{1,0:T(8,128)(2,1)} %get-tuple-element.47.refs_0_, bf16[1536,2048]{1,0:T(8,128)(2,1)} %get-tuple-element.48.refs_1_, ...), custom_call_target="tpu_custom_call" | custom-call | tf_op jit(solution)/shard_map/ffn_bwd_carry/pallas_call | solution.py:663
  224.2 1.4 copy-done.8
  225.6 1.4 copy-done.9
  227.0 22.5 %attn_bwd_carry.1 = (bf16[1536,1536]{1,0:T(8,128)(2,1)}, f32[8,2048]{1,0:T(8,128)S(1)}, f32[32,512]{1,0:T(8,128)S(1)}, f32[8,1536]{1,0:T(8,128)S(1)}, f32[8,512]{1,0:T(8,128)S(1)}) custom-call(bf16[1536,1536]{1,0:T(8,128)(2,1)} %get-tuple-element.43.q_ref.k_ref.v_ref, bf16[1536,1536]{1,0:T(8,128)(2,1)} %get-tuple-element.43.q_ref.k_ref.v_ref, ...), custom_call_target="tpu_custom_call" | custom-call | tf_op jit(solution)/shard_map/attn_bwd_carry/pallas_call | solution.py:727
  249.5 4.9 %fusion.7 = f32[512,1536]{1,0:T(8,128)S(1)} fusion(bf16[1536,512]{1,0:T(8,128)(2,1)S(1)} %copy-done.18, bf16[1536,1536]{1,0:T(8,128)(2,1)} %get-tuple-element.68), kind=kOutput, calls=%fused_computation.24 | convolution fusion | flops 2415919104 | bytes 9437184 | tf_op jit(solution)/shard_map/dot_general | solution.py:29
  254.6 43.6 %reduce_grads.1 = (f32[8,2048]{1,0:T(8,128)S(1)}, f32[32,512]{1,0:T(8,128)S(1)}, f32[8,1536]{1,0:T(8,128)S(1)}, f32[8,512]{1,0:T(8,128)S(1)}) custom-call(f32[4,4,4,8,2048]{4,3,2,1,0:T(8,128)S(1)} %bitcast.51, f32[4,4,4,32,512]{4,3,2,1,0:T(8,128)S(1)} %bitcast.50, f32[4,4,4,8,1536]{4,3,2,1,0:T(8,128)S(1)} %bitcast.52, f32[4,4,4,8,512]{4,3,2,1,0:T(8,128)S(1)} %bitcast.54), custom_call_target="tpu_custom_call" | custom-call | tf_op jit(solution)/shard_map/reduce_grads/pallas_call | solution.py:551
  298.8 0.7 reshape.119
  299.5 0.6 select_bitcast_fusion
  300.2 0.6 select_bitcast_fusion.1
  300.8 1.4 broadcast_select_fusion.1
  302.3 1.3 pad_maximum_fusion
  (38 shorter events, 1.6 us)
Async XLA Ops:
  1.5 3.8 %copy-start.12 = (bf16[1,8,2048]{2,1,0:T(8,128)(2,1)S(1)}, bf16[1,8,2048]{2,1,0:T(8,128)(2,1)}, u32[]{:S(2)}) copy-start(bf16[1,8,2048]{2,1,0:T(8,128)(2,1)} %param.10) | copy-start | bytes 98308
  1.6 3.8 %copy-start.13 = (bf16[1,32,512]{2,1,0:T(8,128)(2,1)S(1)}, bf16[1,32,512]{2,1,0:T(8,128)(2,1)}, u32[]{:S(2)}) copy-start(bf16[1,32,512]{2,1,0:T(8,128)(2,1)} %param.11) | copy-start | bytes 98308
  1.6 3.8 %copy-start.14 = (bf16[1,8,512]{2,1,0:T(8,128)(2,1)S(1)}, bf16[1,8,512]{2,1,0:T(8,128)(2,1)}, u32[]{:S(2)}) copy-start(bf16[1,8,512]{2,1,0:T(8,128)(2,1)} %param.9) | copy-start | bytes 24580
  49.2 2.0 copy-start
  51.2 2.0 copy-start.1
  53.2 1.6 copy-start.2
  54.8 1.0 copy-start.4
  102.2 18.5 %copy-start.3 = (bf16[2,4,4,4,8,1536]{5,4,3,2,1,0:T(8,128)(2,1)S(1)}, bf16[2,4,4,4,8,1536]{5,4,3,2,1,0:T(8,128)(2,1)}, u32[]{:S(2)}) copy-start(bf16[2,4,4,4,8,1536]{5,4,3,2,1,0:T(8,128)(2,1)} %copy-done.2) | copy-start | bytes 9437188
  120.3 180.5 %collective-permute-start = (bf16[4,1,192,512]{3,2,1,0:T(8,128)(2,1)}, bf16[4,1,192,512]{3,2,1,0:T(8,128)(2,1)}, u32[]{:S(2)}, u32[]{:S(2)}) collective-permute-start(bf16[4,1,192,512]{3,2,1,0:T(8,128)(2,1)} %constant_dynamic-slice_fusion), channel_id=1, source_target_pairs={{0,64},{64,0},{1,65},{65,1},{2,66},{66,2},{3,67},{67,3},{4,68},{68... | collective-permute-start | bytes 2359304 | tf_op jit(solution)/shard_map/ppermute | solution.py:782
  120.7 1.7 copy-start.5
  146.8 1.0 copy-start.10
  147.8 19.2 %copy-start.15 = (bf16[1536,512]{1,0:T(8,128)(2,1)S(1)}, bf16[1536,512]{1,0:T(8,128)(2,1)}, u32[]{:S(2)}) copy-start(bf16[1536,512]{1,0:T(8,128)(2,1)} %get-tuple-element.49.h_ref) | copy-start | bytes 4718596
  167.0 5.8 %copy-start.16 = (bf16[1536,1536]{1,0:T(8,128)(2,1)S(1)}, bf16[1536,1536]{1,0:T(8,128)(2,1)}, u32[]{:S(2)}) copy-start(bf16[1536,1536]{1,0:T(8,128)(2,1)} %attn_bwd.1) | copy-start | bytes 14155780
  167.0 5.8 %copy-start.19 = (bf16[1536,512]{1,0:T(8,128)(2,1)S(1)}, bf16[1536,512]{1,0:T(8,128)(2,1)}, u32[]{:S(2)}) copy-start(bf16[1536,512]{1,0:T(8,128)(2,1)} %get-tuple-element.61) | copy-start | bytes 4718596
  224.2 1.4 copy-start.8
  225.6 1.4 copy-start.9
  227.0 22.5 %copy-start.18 = (bf16[1536,512]{1,0:T(8,128)(2,1)S(1)}, bf16[1536,512]{1,0:T(8,128)(2,1)}, u32[]{:S(2)}) copy-start(bf16[1536,512]{1,0:T(8,128)(2,1)} %get-tuple-element.65) | copy-start | bytes 4718596
  249.5 5.0 %copy-start.6 = (f32[2048,512]{1,0:T(8,128)S(1)}, f32[2048,512]{1,0:T(8,128)}, u32[]{:S(2)}) copy-start(f32[2048,512]{1,0:T(8,128)} %get-tuple-element.64) | copy-start | bytes 12582916
  249.5 5.0 %copy-start.7 = (f32[512,2048]{1,0:T(8,128)S(1)}, f32[512,2048]{1,0:T(8,128)}, u32[]{:S(2)}) copy-start(f32[512,2048]{1,0:T(8,128)} %get-tuple-element.63) | copy-start | bytes 12582916
  249.5 5.1 %copy-start.11 = (f32[512,512]{1,0:T(8,128)S(1)}, f32[512,512]{1,0:T(8,128)}, u32[]{:S(2)}) copy-start(f32[512,512]{1,0:T(8,128)} %get-tuple-element.69) | copy-start | bytes 3145732
  254.6 46.2 %copy-start.17 = (bf16[1536,512]{1,0:T(8,128)(2,1)S(1)}, bf16[1536,512]{1,0:T(8,128)(2,1)}, u32[]{:S(2)}) copy-start(bf16[1536,512]{1,0:T(8,128)(2,1)} %get-tuple-element.78) | copy-start | bytes 4718596
where the time goes:
time: 308 us; the launch traced here: 304 us
  Pallas kernels  261 us (85%)
  local copies, waits for them, and re-layouts  19.7 us (6%)
  matrix products  15 us (5%)
  other arithmetic  6.55 us (2%)
    pallas_call x2, Pallas kernels, ffn_bwd(): pl.pallas_call(functools.partial(ffn_bwd_kernel, tile, carry), grid=(ff /...  69.5 us
    pallas_call x1, Pallas kernels, gather_weights(): pl.pallas_call(gather_kernel, in_specs=[vmem] * 4, out_specs=[vmem] * 4,...  43.8 us
    pallas_call x1, Pallas kernels, reduce_grads(): pl.pallas_call(reduce_kernel, in_specs=[pl.BlockSpec(memory_space=pl.ANY)...  43.6 us
    pallas_call x2, Pallas kernels, attn_bwd(): pl.pallas_call(functools.partial(kernel, scale, width), grid=(tokens // s...  41.7 us
    pallas_call x2, Pallas kernels, post_attn(): pl.pallas_call(post_kernel, grid=(tokens // tile,), in_specs=[row(d), row...  31.6 us
    pallas_call x2, Pallas kernels, attn_fwd(): pl.pallas_call(functools.partial(attn_fwd_kernel, scale), grid=(tokens //...  17.5 us
    pallas_call x2, Pallas kernels, pre_attn(): pl.pallas_call(pre_kernel, grid=(tokens // tile,), in_specs=[row(d), whol...  13.3 us
    unnamed x40, local copies, waits for them, and re-layouts  10.8 us
  transfers between devices with their start and end apart: 1, of which 0 were waited for; matrix products, arithmetic and copies ran while one was open for 7% of the time, Pallas kernels for 51%

commit v1 on v0

--- a/solution.py
+++ b/solution.py
@@ -105,18 +105,18 @@
 
 def attn_fwd(qkv, seq, scale):
     tokens, width = qkv.shape[0], qkv.shape[1] // 3
-    spec = lambda off: pl.BlockSpec((seq, width), lambda b: (b, off))
+    spec = lambda off: pl.BlockSpec((seq, width // 2), lambda b, j: (b, off + j))
     return pl.pallas_call(
         functools.partial(attn_fwd_kernel, scale),
-        grid=(tokens // seq,),
-        in_specs=[spec(0), spec(1), spec(2)],
+        grid=(tokens // seq, 2),
+        in_specs=[spec(0), spec(2), spec(4)],
         out_specs=spec(0),
         out_shape=jax.ShapeDtypeStruct((tokens, width), BF),
         name="attn_fwd",
     )(qkv, qkv, qkv)
 
 
-def pre_kernel(h_ref, w_ref, n_ref, qkv_ref):
+def pre_kernel(_, h_ref, w_ref, n_ref, qkv_ref):
     normed = rms_norm(h_ref[...].astype(F32)).astype(BF)
     n_ref[...] = normed
     qkv_ref[...] = dot(normed, w_ref[...]).astype(BF)
@@ -128,49 +128,58 @@
     return pl.BlockSpec(block, lambda *_: index, pipeline_mode=pl.Buffered(1))
 
 
-def pre_attn(hidden, w_qkv, layer, tile):
-    tokens, d = hidden.shape
+def rows_at(tile, n, shifted=False):
+    return pl.BlockSpec((tile, n), lambda i, first: (i + first[0] if shifted else i, 0))
+
+
+def pre_attn(hidden, first, tokens, w_qkv, layer, tile):
+    d = hidden.shape[1]
     cols = w_qkv.shape[2]
-    row = lambda n: pl.BlockSpec((tile, n), lambda i: (i, 0))
     return pl.pallas_call(
         pre_kernel,
-        grid=(tokens // tile,),
-        in_specs=[row(d), whole((d, cols), layer)],
-        out_specs=[row(d), row(cols)],
+        grid_spec=pltpu.PrefetchScalarGridSpec(
+            num_scalar_prefetch=1, grid=(tokens // tile,),
+            in_specs=[rows_at(tile, d, True), whole((d, cols), layer)],
+            out_specs=[rows_at(tile, d), rows_at(tile, cols)]),
         out_shape=[jax.ShapeDtypeStruct((tokens, d), BF), jax.ShapeDtypeStruct((tokens, cols), BF)],
         name="pre_attn",
-    )(hidden, w_qkv)
-
-
-def post_kernel(h_ref, a_ref, wp_ref, wu_ref, wd_ref, mid_ref, n2_ref, up_ref, ge_ref, out_ref):
+    )(first, hidden, w_qkv)
+
+
+def post_kernel(_, h_ref, a_ref, wp_ref, wu_ref, wd_ref, mid_ref, n2_ref, up_ref, ge_ref, out_ref):
     mid = (h_ref[...].astype(F32) + dot(a_ref[...], wp_ref[...])).astype(BF)
     mid_ref[...] = mid
     mid_f32 = mid.astype(F32)
     n2 = rms_norm(mid_f32).astype(BF)
     n2_ref[...] = n2
     ff = wu_ref.shape[1]
-    for c in range(0, ff, 512):
-        up = dot(n2, wu_ref[:, c:c + 512]).astype(BF)
-        up_ref[:, c:c + 512] = up
+
+    def chunk(c, _):
+        cols = pl.ds(pl.multiple_of(c * 512, 512), 512)
+        up = dot(n2_ref[...], wu_ref[:, cols]).astype(BF)
+        up_ref[:, cols] = up
         u = up.astype(F32)
         t = jnp.tanh(u * (GELU_A + GELU_B * (u * u)))
-        ge_ref[:, c:c + 512] = (u * (0.5 * t + 0.5)).astype(BF)
+        ge_ref[:, cols] = (u * (0.5 * t + 0.5)).astype(BF)
+        return 0
+
+    lax.fori_loop(0, ff // 512, chunk, 0)
     out_ref[...] = (mid_f32 + dot(ge_ref[...], wd_ref[...])).astype(BF)
 
 
-def post_attn(hidden, attn, w_proj, w_up, w_down, layer, tile):
-    tokens, d = hidden.shape
+def post_attn(hidden, first, attn, w_proj, w_up, w_down, layer, tile):
+    tokens, d = attn.shape
     ff = w_up.shape[2]
-    row = lambda n: pl.BlockSpec((tile, n), lambda i: (i, 0))
     sizes = (d, d, ff, ff, d)
     return pl.pallas_call(
         post_kernel,
-        grid=(tokens // tile,),
-        in_specs=[row(d), row(d), whole((d, d), layer), whole((d, ff), layer), whole((ff, d), layer)],
-        out_specs=[row(n) for n in sizes],
+        grid_spec=pltpu.PrefetchScalarGridSpec(
+            num_scalar_prefetch=1, grid=(tokens // tile,),
+            in_specs=[rows_at(tile, d, True), rows_at(tile, d), whole((d, d), layer), whole((d, ff), layer), whole((ff, d), layer)],
+            out_specs=[rows_at(tile, n) for n in sizes]),
         out_shape=[jax.ShapeDtypeStruct((tokens, n), BF) for n in sizes],
         name="post_attn",
-    )(hidden, attn, w_proj, w_up, w_down)
+    )(first, hidden, attn, w_proj, w_up, w_down)
 
 
 def gelu_pull(u, g):
@@ -213,109 +222,101 @@
     return copy
 
 
-def gather_kernel(up_ref, down_ref, qkv_ref, proj_ref, wup, wdown, wqkv, wproj, local_sem, send_sem, recv_sem, psend_sem, precv_sem):
+def gather_kernel(up_ref, down_ref, qkv_ref, proj_ref, *rest):
+    results, bufs, (local_sem, send_sem, recv_sem, psend_sem, precv_sem, out_sem) = rest[:4], rest[4:8], rest[8:]
     pp = lax.axis_index("pp")
     partner = 1 - pp
     me = tuple(lax.axis_index(a) for a in AXES)
-    arrays = ((0, up_ref, wup), (1, down_ref, wdown), (2, qkv_ref, wqkv), (2, proj_ref, wproj))
-
-    def half_of(ref, half):
-        rows, cols = ref.shape[-2:]
-        lead = (slice(None),) * (len(ref.shape) - 2)
-        if rows > 8:
-            return ref.at[lead + (pl.ds(half * (rows // 2), rows // 2), slice(None))]
-        return ref.at[lead + (slice(None), pl.ds(half * (cols // 2), cols // 2))]
-
-    def block(n, phase, where):
-        group, _, out = arrays[n]
-        order = GATHER_ORDER[group]
+    sources = (up_ref, down_ref, qkv_ref, proj_ref)
+    groups = (0, 1, 2, 2)
+
+    def region(base, n, phase, by, half, layer):
+        order = GATHER_ORDER[groups[n]]
         idx = [None, None, None]
         for later, axis in enumerate(order):
-            idx[axis] = slice(None) if later < phase else (where if later == phase else me[axis])
-        return out.at[(pp,) + tuple(idx)]
-
-    for n, (_, src, out) in enumerate(arrays):
-        pltpu.make_async_copy(src, out.at[(pp,) + me], local_sem.at[n]).start()
+            idx[axis] = slice(None) if later < phase else step_coord(me[axis], by if later == phase else 0)
+        rows, cols = base[n].shape[-2:]
+        tail = (slice(None), slice(None))
+        if half is not None and rows > 8:
+            tail = (pl.ds(half * (rows // 2), rows // 2), slice(None))
+        elif half is not None:
+            tail = (slice(None), pl.ds(half * (cols // 2), cols // 2))
+        return base[n].at[(layer,) + tuple(idx) + tail]
+
+    own = [pltpu.make_async_copy(src, bufs[n].at[(pp,) + me], local_sem.at[n]) for n, src in enumerate(sources)]
+    for copy in own:
+        copy.start()
     enter(me, partner)
-    for n, (_, src, out) in enumerate(arrays):
-        pltpu.make_async_copy(src, out.at[(pp,) + me], local_sem.at[n]).wait()
-
-    sends = []
-    partners = []
-
-    def tell_partner(ref, n, slot):
+    for copy in own:
+        copy.wait()
+
+    sends, partners, locals_ = [], [], []
+
+    def put_out(n, slot, by, half, layer, side):
+        copy = pltpu.make_async_copy(region(bufs, n, 2, by, half, layer), region(results, n, 2, by, half, layer), out_sem.at[n, slot, side])
+        copy.start()
+        locals_.append(copy)
+
+    def ready(n, slot, by, half):
+        ref = region(bufs, n, 2, by, half, pp)
         copy = remote(ref, ref, psend_sem.at[n, slot], precv_sem.at[n, slot], {"pp": partner})
-        partners.append(copy)
-
-    def send(ref, n, phase, slot, by):
-        axis = GATHER_ORDER[arrays[n][0]][phase]
-        copy = remote(ref, ref, send_sem.at[n, phase, slot], recv_sem.at[n, phase, slot], neighbour(me, axis, by))
-        sends.append(copy)
-
-    def arrived(ref, n, phase, slot):
+        partners.append((copy, n, slot, by, half))
+        put_out(n, slot, by, half, pp, 0)
+
+    def send(n, phase, slot, by, half, to):
+        axis = GATHER_ORDER[groups[n]][phase]
+        ref = region(bufs, n, phase, by, half, pp)
+        sends.append(remote(ref, ref, send_sem.at[n, phase, slot], recv_sem.at[n, phase, slot], neighbour(me, axis, to)))
+
+    def arrived(n, phase, slot, by, half):
+        ref = region(bufs, n, phase, by, half, pp)
         pltpu.make_async_copy(ref, ref, recv_sem.at[n, phase, slot]).wait()
+        if phase == 2:
+            ready(n, slot + 1, by, half)
 
     for phase in range(3):
-        last = phase == 2
-        place = [me[GATHER_ORDER[arrays[n][0]][phase]] for n in range(4)]
         for n in range(4):
-            mine = block(n, phase, place[n])
-            send(half_of(mine, 0), n, phase, 0, 1)
-            send(half_of(mine, 1), n, phase, 1, 3)
+            send(n, phase, 0, 0, 0, 1)
+            send(n, phase, 1, 0, 1, 3)
         for n in range(4):
-            mine = block(n, phase, place[n])
-            send(half_of(mine, 1), n, phase, 2, 1)
-            send(half_of(mine, 0), n, phase, 3, 3)
-            if last:
-                tell_partner(mine, n, 0)
+            send(n, phase, 2, 0, 1, 1)
+            send(n, phase, 3, 0, 0, 3)
+            if phase == 2:
+                ready(n, 0, 0, None)
         for n in range(4):
-            left = block(n, phase, step_coord(place[n], 3))
-            right = block(n, phase, step_coord(place[n], 1))
-            arrived(half_of(left, 0), n, phase, 0)
-            send(half_of(left, 0), n, phase, 4, 1)
-            if last:
-                tell_partner(half_of(left, 0), n, 1)
-            arrived(half_of(right, 1), n, phase, 1)
-            send(half_of(right, 1), n, phase, 5, 3)
-            if last:
-                tell_partner(half_of(right, 1), n, 2)
+            arrived(n, phase, 0, 3, 0)
+            send(n, phase, 4, 3, 0, 1)
+            arrived(n, phase, 1, 1, 1)
+            send(n, phase, 5, 1, 1, 3)
         for n in range(4):
-            left = block(n, phase, step_coord(place[n], 3))
-            right = block(n, phase, step_coord(place[n], 1))
-            arrived(half_of(left, 1), n, phase, 2)
-            if last:
-                tell_partner(half_of(left, 1), n, 3)
-            arrived(half_of(right, 0), n, phase, 3)
-            if last:
-                tell_partner(half_of(right, 0), n, 4)
+            arrived(n, phase, 2, 3, 1)
+            arrived(n, phase, 3, 1, 0)
         for n in range(4):
-            far = block(n, phase, step_coord(place[n], 2))
-            arrived(half_of(far, 0), n, phase, 4)
-            if last:
-                tell_partner(half_of(far, 0), n, 5)
-            arrived(half_of(far, 1), n, phase, 5)
-            if last:
-                tell_partner(half_of(far, 1), n, 6)
+            arrived(n, phase, 4, 2, 0)
+            arrived(n, phase, 5, 2, 1)
+    for copy, n, slot, by, half in partners:
+        copy.wait_recv()
+        put_out(n, slot, by, half, partner, 1)
     for copy in sends:
         copy.wait_send()
-    for copy in partners:
+    for copy, *_ in partners:
         copy.wait_send()
-    for copy in partners:
-        copy.wait_recv()
+    for copy in locals_:
+        copy.wait()
 
 
 def gather_weights(w_qkv, w_proj, w_up, w_down):
     vmem = pl.BlockSpec(memory_space=pltpu.VMEM)
-    full = lambda w: jax.ShapeDtypeStruct((2, 4, 4, 4) + w.shape, BF)
+    shape = lambda w: (2, 4, 4, 4) + w.shape
     dma = pltpu.SemaphoreType.DMA
     args = (w_up, w_down, w_qkv, w_proj)
     outs = pl.pallas_call(
         gather_kernel,
         in_specs=[vmem] * 4,
-        out_specs=[vmem] * 4,
-        out_shape=[full(w) for w in args],
-        scratch_shapes=[dma((4,)), dma((4, 3, 6)), dma((4, 3, 6)), dma((4, 7)), dma((4, 7))],
-        compiler_params=pltpu.CompilerParams(collective_id=0, has_side_effects=True, vmem_limit_bytes=40 << 20),
+        out_specs=[pl.BlockSpec(memory_space=pltpu.HBM)] * 4,
+        out_shape=[jax.ShapeDtypeStruct(shape(w), BF) for w in args],
+        scratch_shapes=[pltpu.VMEM(shape(w), BF) for w in args] + [dma((4,)), dma((4, 3, 6)), dma((4, 3, 6)), dma((4, 7)), dma((4, 7)), dma((4, 7, 2))],
+        compiler_params=pltpu.CompilerParams(collective_id=0, has_side_effects=True, vmem_limit_bytes=62 << 20),
         name="gather_weights",
     )(*args)
     flat = [o.reshape(2, -1, o.shape[-1]) for o in outs]
@@ -339,32 +340,15 @@
 
 
 def add_block(out, dst, src):
-    dims = dst.shape[:-2]
-    total = 1
-    for s in dims:
-        total *= s
-
-    def spread(flat, inner):
-        index = []
-        for s in reversed(inner):
-            index.append(flat % s)
-            flat //= s
-        return tuple(reversed(index))
-
-    def one(index):
-        out[index] = dst[index] + src[index]
-
-    if total <= 4:
-        for flat in range(total):
-            one(spread(flat, dims))
+    if len(dst.shape) < 4:
+        out[...] = dst[...] + src[...]
         return
 
     def body(i, _):
-        for flat in range(total // dims[0]):
-            one((i,) + spread(flat, dims[1:]))
+        out[i] = dst[i] + src[i]
         return 0
 
-    lax.fori_loop(0, dims[0], body, 0)
+    lax.fori_loop(0, dst.shape[0], body, 0)
 
 
 class Reducer:
@@ -430,6 +414,12 @@
         for n in {2: (0, 1), 1: (2,), 3: (3,), 0: ()}[by]:
             self.copy(color, phase, n).start()
 
+    def start_swaps(self, refs, peer, swap_sems, pos):
+        if pos < 4:
+            for color in range(3):
+                for copy in self.swaps(refs, peer, swap_sems, color, pos):
+                    copy.start()
+
     def swapped(self, refs, peer, load_sem, swap_sems, pos):
         by = REDUCE_OFFSETS[pos]
         for color in range(3):
@@ -437,6 +427,8 @@
                 copy.wait()
             for copy in self.swaps(refs, peer, swap_sems, color, pos):
                 copy.wait_recv()
+        self.start_swaps(refs, peer, swap_sems, pos + 1)
+        for color in range(3):
             block = self.acc.at[(color,) + self.lead(color, 0, self.place(color, 0, by))]
             add_block(block, block, peer.at[(color,) + self.lead(color, 0, self.place(color, 0, by))])
             self.first_sends(color, 0, by)
@@ -507,10 +499,7 @@
             for copy in red.loads(refs, load_sem, color, pos):
                 copy.start()
     enter(red.me, red.partner)
-    for pos in range(4):
-        for color in range(3):
-            for copy in red.swaps(refs, peer, swap_sems, color, pos):
-                copy.start()
+    red.start_swaps(refs, peer, swap_sems, 0)
     for pos in range(4):
         red.swapped(refs, peer, load_sem, swap_sems, pos)
     for phase in range(3):
@@ -561,6 +550,8 @@
 
 
 def ffn_bwd_kernel(tile, carry, *refs):
+    if not carry:
+        refs = refs[1:]
     ge_ref, up_ref, ct_ref, n2_ref, mid_ref, at_ref, wd_ref, wu_ref, wp_ref = refs[:9]
     refs = refs[9:]
     step = pl.program_id(0)
@@ -585,8 +576,7 @@
         for copy in every(lambda color, pos: red.loads(grads, load_sem, color, pos)):
             copy.start()
         enter(red.me, red.partner)
-        for copy in every(lambda color, pos: red.swaps(grads, peer, swap_sems, color, pos)):
-            copy.start()
+        red.start_swaps(grads, peer, swap_sems, 0)
 
     def finish():
         red.fourth(0, reduced)
@@ -602,9 +592,11 @@
         if carry:
             todo = {
                 0: begin,
-                1: lambda: swapped(0, 1, 2, 3),
-                2: lambda: red.second(0),
-                3: lambda: red.third(0),
+                1: lambda: swapped(0),
+                2: lambda: swapped(1),
+                3: lambda: swapped(2),
+                4: lambda: (swapped(3), red.second(0))[0],
+                6: lambda: red.third(0),
             }
             for k, f in todo.items():
                 at(k, f)
@@ -638,15 +630,16 @@
         at(last, finish)
 
 
-def ffn_bwd(gelu, up, ct, normed2, mid, attn, w_down, w_up, w_proj, layer, tile, carried):
-    tokens, d = ct.shape
+def ffn_bwd(gelu, up, ct, first, normed2, mid, attn, w_down, w_up, w_proj, layer, tile, carried):
+    tokens, d = mid.shape
     ff = gelu.shape[1]
-    part = 512
+    part = 256
     act = whole((tokens, d))
-    cols = pl.BlockSpec((tokens, part), lambda i: (0, i))
-    in_specs = [cols, cols, act, act, act, act,
-                pl.BlockSpec((None, part, d), lambda i: (layer, i, 0)), pl.BlockSpec((None, d, part), lambda i: (layer, 0, i)), whole((d, d), layer)]
-    out_specs = [pl.BlockSpec((part, d), lambda i: (i, 0)), pl.BlockSpec((d, part), lambda i: (0, i)), whole((d, d)), act, act]
+    cols = pl.BlockSpec((tokens, part), lambda i, *_: (0, i))
+    ct_spec = act if carried is not None else pl.BlockSpec((tokens, d), lambda i, first: (first[0], 0), pipeline_mode=pl.Buffered(1))
+    in_specs = [cols, cols, ct_spec, act, act, act,
+                pl.BlockSpec((None, part, d), lambda i, *_: (layer, i, 0)), pl.BlockSpec((None, d, part), lambda i, *_: (layer, 0, i)), whole((d, d), layer)]
+    out_specs = [pl.BlockSpec((part, d), lambda i, *_: (i, 0)), pl.BlockSpec((d, part), lambda i, *_: (0, i)), whole((d, d)), act, act]
     out_shape = [jax.ShapeDtypeStruct((ff, d), F32), jax.ShapeDtypeStruct((d, ff), F32), jax.ShapeDtypeStruct((d, d), F32),
                  jax.ShapeDtypeStruct((tokens, d), BF), jax.ShapeDtypeStruct((tokens, d), BF)]
     scratch = [VMEM((tokens, d), F32), VMEM((tokens, part), BF)]
@@ -655,6 +648,7 @@
     carry = carried is not None
     if carry:
         args = args + tuple(grad_views(carried))
+        first = None
         in_specs = in_specs + [pl.BlockSpec(memory_space=pl.ANY)] * 4
         out_specs = out_specs + [whole((3, 4, 4, 2, 8, 512))]
         out_shape = out_shape + [jax.ShapeDtypeStruct((3, 4, 4, 2, 8, 512), F32)]
@@ -662,10 +656,12 @@
         params = dict(vmem_limit_bytes=62 << 20, collective_id=2, has_side_effects=True)
     return pl.pallas_call(
         functools.partial(ffn_bwd_kernel, tile, carry),
-        grid=(ff // part,), in_specs=in_specs, out_specs=out_specs, out_shape=out_shape, scratch_shapes=scratch,
+        grid_spec=pltpu.PrefetchScalarGridSpec(
+            num_scalar_prefetch=0 if carry else 1, grid=(ff // part,), in_specs=in_specs, out_specs=out_specs, scratch_shapes=scratch),
+        out_shape=out_shape,
         compiler_params=pltpu.CompilerParams(**params),
         name="ffn_bwd_carry" if carry else "ffn_bwd",
-    )(*args)
+    )(*(args if carry else (first,) + args))
 
 
 def attn_carry_kernel(scale, width, q_ref, k_ref, v_ref, do_ref, acc_hbm, dqkv_ref, *rest):
@@ -732,18 +728,18 @@
     )(*args)
 
 
-def layer_forward(hidden, weights, layer, seq, scale):
+def layer_forward(hidden, first, tokens, weights, layer, seq, scale):
     w_qkv, w_proj, w_up, w_down = weights
-    normed, qkv = pre_attn(hidden, w_qkv, layer, seq)
+    normed, qkv = pre_attn(hidden, first, tokens, w_qkv, layer, seq)
     attn = attn_fwd(qkv, seq, scale)
-    mid, normed2, up, gelu, out = post_attn(hidden, attn, w_proj, w_up, w_down, layer, seq)
+    mid, normed2, up, gelu, out = post_attn(hidden, first, attn, w_proj, w_up, w_down, layer, seq)
     return out, (hidden, normed, qkv, attn, mid, normed2, up, gelu)
 
 
-def layer_backward(saved, ct_out, weights, layer, seq, scale, carried):
+def layer_backward(saved, ct_out, first, weights, layer, seq, scale, carried):
     w_qkv, w_proj, w_up, w_down = weights
     hidden, normed, qkv, attn, mid, normed2, up, gelu = saved
-    res = ffn_bwd(gelu, up, ct_out, normed2, mid, attn, w_down, w_up, w_proj, layer, seq, carried)
+    res = ffn_bwd(gelu, up, ct_out, first, normed2, mid, attn, w_down, w_up, w_proj, layer, seq, carried)
     g_down, g_up, g_proj, ct_mid, ct_attn = res[:5]
     res = attn_bwd(qkv, ct_attn, seq, scale, res[5] if carried is not None else None)
     ct_qkv = res[0]
@@ -770,10 +766,11 @@
         scale = hd ** -0.5
 
         full = gather_weights(*(w.reshape(w.shape[1], -1) for w in (w_qkv, w_proj, w_up, w_down)))
-        act = lax.dynamic_slice_in_dim(act_in, pp * mine, mine, 0).reshape(mine * seq, d)
-        seed = lax.dynamic_slice_in_dim(loss_seed, pp * mine, mine, 0).reshape(mine * seq, d)
-        h1, saved0 = layer_forward(act, full, 0, seq, scale)
-        h2, saved1 = layer_forward(h1, full, 1, seq, scale)
+        tokens = mine * seq
+        act, seed = act_in.reshape(micro * seq, d), loss_seed.reshape(micro * seq, d)
+        pp_vec, none = jnp.full((1,), pp, jnp.int32), jnp.zeros((1,), jnp.int32)
+        h1, saved0 = layer_forward(act, pp_vec * mine, tokens, full, 0, seq, scale)
+        h2, saved1 = layer_forward(h1, none, tokens, full, 1, seq, scale)
 
         out4 = h2.reshape(mine, 1, seq, d)
         half = seq // 2
@@ -782,8 +779,8 @@
         got = lax.ppermute(give, 'pp', swap)
         act_out = jnp.concatenate([jnp.where(pp == 0, keep, got), jnp.where(pp == 0, got, keep)], axis=0)
 
-        grads1, ct1 = layer_backward(saved1, seed, full, 1, seq, scale, None)
-        grads0, red1 = layer_backward(saved0, ct1, full, 0, seq, scale, grads1)
+        grads1, ct1 = layer_backward(saved1, seed, pp_vec, full, 1, seq, scale, None)
+        grads0, red1 = layer_backward(saved0, ct1, None, full, 0, seq, scale, grads1)
         red0 = reduce_grads(grads0, 0)
         outs = [jnp.where(pp == 0, a, b) for a, b in zip(red0, red1)]
         return tuple(o.reshape(w.shape) for o, w in zip(outs, (w_qkv, w_proj, w_up, w_down))) + (act_out,)

time: 308 us -> 300 us (0.974); the launches traced: 304 us -> 299 us
  local copies, waits for them, and re-layouts: 19.7 us -> 11.2 us
  Pallas kernels: 261 us -> 266 us
    unnamed x40 -> x28, local copies, waits for them, and re-layouts: 10.8 us -> 5.33 us
    dynamic_slice x1 -> x0, local copies, waits for them, and re-layouts: 3.81 us -> none  [device_step(): lax.dynamic_slice_in_dim(loss_seed, pp * mine, mine, 0)]
  transfers between devices with their start and end apart: 1 -> 1, of which waited for: 0 -> 0; matrix products, arithmetic and copies ran while one was open for 7% -> 7% of each run, Pallas kernels for 51% -> 50%
where the time goes in v1:
time: 300 us; the launch traced here: 299 us
  Pallas kernels  266 us (89%)
  matrix products  14.3 us (5%)
  local copies, waits for them, and re-layouts  11.2 us (4%)
  other arithmetic  6.6 us (2%)
    pallas_call x2, Pallas kernels, ffn_bwd(): pl.pallas_call(functools.partial(ffn_bwd_kernel, tile, carry), grid_spec=...  62.4 us
    pallas_call x1, Pallas kernels, gather_weights(): pl.pallas_call(gather_kernel, in_specs=[vmem] * 4, out_specs=[pl.BlockSpe...  45.6 us
    pallas_call x1, Pallas kernels, reduce_grads(): pl.pallas_call(reduce_kernel, in_specs=[pl.BlockSpec(memory_space=pl.ANY)...  44.6 us
    pallas_call x2, Pallas kernels, attn_bwd(): pl.pallas_call(functools.partial(kernel, scale, width), grid=(tokens // s...  42.3 us
    pallas_call x2, Pallas kernels, post_attn(): pl.pallas_call(post_kernel, grid_spec=pltpu.PrefetchScalarGridSpec(num_sc...  37.5 us
    pallas_call x2, Pallas kernels, attn_fwd(): pl.pallas_call(functools.partial(attn_fwd_kernel, scale), grid=(tokens //...  20.4 us
    pallas_call x2, Pallas kernels, pre_attn(): pl.pallas_call(pre_kernel, grid_spec=pltpu.PrefetchScalarGridSpec(num_sca...  13.3 us
    dot_general x2, matrix products, dot_tn(): lax.dot_general(a, b, (((0,), (0,)), ((), ())), preferred_element_type=F32)  9.02 us
  transfers between devices with their start and end apart: 1, of which 0 were waited for; matrix products, arithmetic and copies ran while one was open for 7% of the time, Pallas kernels for 50%

profile of v1, /device:TPU:1, one launch (start us, length us, event | category | flops | bytes accessed | tf_op | source)
XLA Modules:
  0.0 299.2 jit_solution(9898681327753025011)
XLA Ops:
  0.6 1.5 reshape.104.qkv_ref
  2.2 45.6 %gather_weights.1 = (bf16[2,4,4,4,8,2048]{5,4,3,2,1,0:T(8,128)(2,1)}, bf16[2,4,4,4,32,512]{5,4,3,2,1,0:T(8,128)(2,1)}, bf16[2,4,4,4,8,1536]{5,4,3,2,1,0:T(8,128)(2,1)}, bf16[2,4,4,4,8,512]{5,4,3,2,1,0:T(8,128)(2,1)}) custom-call(bf16[8,2048]{1,0:T(8,128)(2,1)} %bitcast.65, bf16[32,512]{1,0:T(8,128)(2,1)} %bitcast.66, bf16[8,1536]{1,0:T(8,128)(2,1)} %reshape.104.qkv_ref, ...), custom_call_target="tpu_custom_call" | custom-call | tf_op jit(solution)/shard_map/gather_weights/pallas_call | solution.py:313
  47.8 6.7 %pre_attn.2 = (bf16[1536,512]{1,0:T(8,128)(2,1)}, bf16[1536,1536]{1,0:T(8,128)(2,1)}) custom-call(s32[1]{0:T(128)S(6)} %mul.55._, bf16[3072,512]{1,0:T(8,128)(2,1)} %bitcast.56, bf16[2,512,1536]{2,1,0:T(8,128)(2,1)} %bitcast.54), custom_call_target="tpu_custom_call" | custom-call | tf_op jit(solution)/shard_map/pre_attn/pallas_call | solution.py:138
  54.5 10.2 %attn_fwd.2.a_ref.refs_5_ = bf16[1536,512]{1,0:T(8,128)(2,1)} custom-call(bf16[1536,1536]{1,0:T(8,128)(2,1)} %get-tuple-element.43.q_ref.k_ref.v_ref, bf16[1536,1536]{1,0:T(8,128)(2,1)} %get-tuple-element.43.q_ref.k_ref.v_ref, bf16[1536,1536]{1,0:T(8,128)(2,1)} %get-tuple-element.43.q_ref.k_ref.v_ref), custom_call_target="tpu_custom_call" | custom-call | tf_op jit(solution)/shard_map/attn_fwd/pallas_call | solution.py:109
  64.7 18.7 %post_attn.2 = (bf16[1536,512]{1,0:T(8,128)(2,1)}, bf16[1536,512]{1,0:T(8,128)(2,1)}, bf16[1536,2048]{1,0:T(8,128)(2,1)}, bf16[1536,2048]{1,0:T(8,128)(2,1)}, bf16[1536,512]{1,0:T(8,128)(2,1)}) custom-call(s32[1]{0:T(128)S(6)} %mul.55._, bf16[3072,512]{1,0:T(8,128)(2,1)} %bitcast.57, bf16[1536,512]{1,0:T(8,128)(2,1)} %attn_fwd.2.a_ref.refs_5_, ...), custom_call_target="tpu_custom_call" | custom-call | tf_op jit(solution)/shard_map/post_attn/pallas_call | solution.py:174
  83.4 6.6 %pre_attn.3 = (bf16[1536,512]{1,0:T(8,128)(2,1)}, bf16[1536,1536]{1,0:T(8,128)(2,1)}) custom-call(s32[1]{0:T(128)} %constant.8.clone.1._, bf16[1536,512]{1,0:T(8,128)(2,1)} %get-tuple-element.49.h_ref, bf16[2,512,1536]{2,1,0:T(8,128)(2,1)} %bitcast.55), custom_call_target="tpu_custom_call" | custom-call | tf_op jit(solution)/shard_map/pre_attn/pallas_call | solution.py:138
  90.0 10.2 %attn_fwd.3.a_ref.refs_6_ = bf16[1536,512]{1,0:T(8,128)(2,1)} custom-call(bf16[1536,1536]{1,0:T(8,128)(2,1)} %get-tuple-element.50.q_ref.k_ref.v_ref, bf16[1536,1536]{1,0:T(8,128)(2,1)} %get-tuple-element.50.q_ref.k_ref.v_ref, bf16[1536,1536]{1,0:T(8,128)(2,1)} %get-tuple-element.50.q_ref.k_ref.v_ref), custom_call_target="tpu_custom_call" | custom-call | tf_op jit(solution)/shard_map/attn_fwd/pallas_call | solution.py:109
  100.2 18.8 %post_attn.3 = (bf16[1536,512]{1,0:T(8,128)(2,1)}, bf16[1536,512]{1,0:T(8,128)(2,1)}, bf16[1536,2048]{1,0:T(8,128)(2,1)}, bf16[1536,2048]{1,0:T(8,128)(2,1)}, bf16[1536,512]{1,0:T(8,128)(2,1)}) custom-call(s32[1]{0:T(128)} %constant.8.clone.1._, bf16[1536,512]{1,0:T(8,128)(2,1)} %get-tuple-element.49.h_ref, bf16[1536,512]{1,0:T(8,128)(2,1)} %attn_fwd.3.a_ref.refs_6_, ...), custom_call_target="tpu_custom_call" | custom-call | tf_op jit(solution)/shard_map/post_attn/pallas_call | solution.py:174
  119.0 2.2 constant_dynamic-slice_fusion
  121.1 0.0 collective-permute-start
  121.1 1.5 slice.4
  122.7 26.5 %ffn_bwd.1 = (f32[2048,512]{1,0:T(8,128)}, f32[512,2048]{1,0:T(8,128)}, f32[512,512]{1,0:T(8,128)S(1)}, bf16[1536,512]{1,0:T(8,128)(2,1)S(1)}, bf16[1536,512]{1,0:T(8,128)(2,1)}) custom-call(s32[1]{0:T(128)} %bitcast.refs_0_, bf16[1536,2048]{1,0:T(8,128)(2,1)} %get-tuple-element.51.refs_1_, bf16[1536,2048]{1,0:T(8,128)(2,1)} %get-tuple-element.52.refs_2_, ...), custom_call_target="tpu_custom_call" | custom-call | tf_op jit(solution)/shard_map/ffn_bwd/pallas_call | solution.py:657
  149.2 1.2 copy-done.5
  150.3 1.0 copy-done.7
  151.3 19.2 %attn_bwd.1 = bf16[1536,1536]{1,0:T(8,128)(2,1)} custom-call(bf16[1536,1536]{1,0:T(8,128)(2,1)} %get-tuple-element.50.q_ref.k_ref.v_ref, bf16[1536,1536]{1,0:T(8,128)(2,1)} %get-tuple-element.50.q_ref.k_ref.v_ref, bf16[1536,1536]{1,0:T(8,128)(2,1)} %get-tuple-element.50.q_ref.k_ref.v_ref, bf16[1536,512]{1,0:T(8,128)(2,1)} %get-tuple-element.56.do_ref), custom_call_target="tpu_custom_call" | custom-call | tf_op jit(solution)/shard_map/attn_bwd/pallas_call | solution.py:723
  170.6 5.3 %fusion.3 = (f32[1536]{0:T(1024)S(1)}, f32[1536]{0:T(1024)S(1)}, bf16[1536,512]{1,0:T(8,128)(2,1)S(1)}) fusion(bf16[1536,512]{1,0:T(8,128)(2,1)S(1)} %copy-done.9, bf16[1536,1536]{1,0:T(8,128)(2,1)} %attn_bwd.1, bf16[512,1536]{1,0:T(8,128)(2,1)S(1)} %bitcast.62), kind=kOutput, calls=%fused_computation.7 | convolution fusion | flops 2421421056 | bytes 9449472 | tf_op jit(solution)/shard_map/dot_general | solution.py:25
  175.9 4.3 %fusion.6 = f32[512,1536]{1,0:T(8,128)} fusion(bf16[1536,512]{1,0:T(8,128)(2,1)S(1)} %copy-done.13, bf16[1536,1536]{1,0:T(8,128)(2,1)S(1)} %copy-done.10), kind=kOutput, calls=%fused_computation.21 | convolution fusion | flops 2415919104 | bytes 9437184 | tf_op jit(solution)/shard_map/dot_general | solution.py:29
  180.3 2.0 fusion.2.refs_2_
  182.2 35.9 %ffn_bwd_carry.1 = (f32[2048,512]{1,0:T(8,128)}, f32[512,2048]{1,0:T(8,128)}, f32[512,512]{1,0:T(8,128)}, bf16[1536,512]{1,0:T(8,128)(2,1)}, bf16[1536,512]{1,0:...) custom-call(bf16[1536,2048]{1,0:T(8,128)(2,1)} %get-tuple-element.47.refs_0_, bf16[1536,2048]{1,0:T(8,128)(2,1)} %get-tuple-element.48.refs_1_, ...), custom_call_target="tpu_custom_call" | custom-call | tf_op jit(solution)/shard_map/ffn_bwd_carry/pallas_call | solution.py:657
  218.1 1.4 copy-done.3
  219.5 1.4 copy-done.4
  220.9 23.1 %attn_bwd_carry.1 = (bf16[1536,1536]{1,0:T(8,128)(2,1)}, f32[8,2048]{1,0:T(8,128)S(1)}, f32[32,512]{1,0:T(8,128)S(1)}, f32[8,1536]{1,0:T(8,128)S(1)}, f32[8,512]{1,0:T(8,128)S(1)}) custom-call(bf16[1536,1536]{1,0:T(8,128)(2,1)} %get-tuple-element.43.q_ref.k_ref.v_ref, bf16[1536,1536]{1,0:T(8,128)(2,1)} %get-tuple-element.43.q_ref.k_ref.v_ref, ...), custom_call_target="tpu_custom_call" | custom-call | tf_op jit(solution)/shard_map/attn_bwd_carry/pallas_call | solution.py:723
  244.1 4.7 %fusion.7 = f32[512,1536]{1,0:T(8,128)S(1)} fusion(bf16[1536,512]{1,0:T(8,128)(2,1)S(1)} %copy-done.12, bf16[1536,1536]{1,0:T(8,128)(2,1)} %get-tuple-element.68), kind=kOutput, calls=%fused_computation.22 | convolution fusion | flops 2415919104 | bytes 9437184 | tf_op jit(solution)/shard_map/dot_general | solution.py:29
  248.9 0.1 copy-done.2
  249.0 0.2 copy-done.8
  249.2 44.6 %reduce_grads.1 = (f32[8,2048]{1,0:T(8,128)S(1)}, f32[32,512]{1,0:T(8,128)S(1)}, f32[8,1536]{1,0:T(8,128)S(1)}, f32[8,512]{1,0:T(8,128)S(1)}) custom-call(f32[4,4,4,8,2048]{4,3,2,1,0:T(8,128)S(1)} %bitcast.42, f32[4,4,4,32,512]{4,3,2,1,0:T(8,128)S(1)} %bitcast.41, f32[4,4,4,8,1536]{4,3,2,1,0:T(8,128)S(1)} %bitcast.43, f32[4,4,4,8,512]{4,3,2,1,0:T(8,128)S(1)} %bitcast.45), custom_call_target="tpu_custom_call" | custom-call | tf_op jit(solution)/shard_map/reduce_grads/pallas_call | solution.py:540
  293.8 0.6 select_bitcast_fusion.2
  294.4 0.7 reshape.119
  295.2 0.6 select_bitcast_fusion
  295.8 0.6 select_bitcast_fusion.1
  296.4 1.4 broadcast_select_fusion.1
  297.9 1.3 pad_maximum_fusion
  (25 shorter events, 0.1 us)
Async XLA Ops:
  119.0 3.7 %copy-start = (bf16[2,4,4,4,8,512]{5,4,3,2,1,0:T(8,128)(2,1)S(1)}, bf16[2,4,4,4,8,512]{5,4,3,2,1,0:T(8,128)(2,1)}, u32[]{:S(2)}) copy-start(bf16[2,4,4,4,8,512]{5,4,3,2,1,0:T(8,128)(2,1)} %get-tuple-element.44) | copy-start | bytes 3145732
  121.1 175.3 %collective-permute-start = (bf16[4,1,192,512]{3,2,1,0:T(8,128)(2,1)}, bf16[4,1,192,512]{3,2,1,0:T(8,128)(2,1)}, u32[]{:S(2)}, u32[]{:S(2)}) collective-permute-start(bf16[4,1,192,512]{3,2,1,0:T(8,128)(2,1)} %constant_dynamic-slice_fusion), channel_id=1, source_target_pairs={{0,64},{64,0},{1,65},{65,1},{2,66},{66,2},{3,67},{67,3},{4,68},{68... | collective-permute-start | bytes 2359304 | tf_op jit(solution)/shard_map/ppermute | solution.py:779
  149.2 1.2 copy-start.5
  150.3 1.0 copy-start.7
  151.3 19.2 %copy-start.9 = (bf16[1536,512]{1,0:T(8,128)(2,1)S(1)}, bf16[1536,512]{1,0:T(8,128)(2,1)}, u32[]{:S(2)}) copy-start(bf16[1536,512]{1,0:T(8,128)(2,1)} %get-tuple-element.49.h_ref) | copy-start | bytes 4718596
  170.6 5.3 %copy-start.10 = (bf16[1536,1536]{1,0:T(8,128)(2,1)S(1)}, bf16[1536,1536]{1,0:T(8,128)(2,1)}, u32[]{:S(2)}) copy-start(bf16[1536,1536]{1,0:T(8,128)(2,1)} %attn_bwd.1) | copy-start | bytes 14155780
  170.6 5.3 %copy-start.13 = (bf16[1536,512]{1,0:T(8,128)(2,1)S(1)}, bf16[1536,512]{1,0:T(8,128)(2,1)}, u32[]{:S(2)}) copy-start(bf16[1536,512]{1,0:T(8,128)(2,1)} %get-tuple-element.61) | copy-start | bytes 4718596
  175.9 4.3 %copy-start.6 = (bf16[1536,512]{1,0:T(8,128)(2,1)S(1)}, bf16[1536,512]{1,0:T(8,128)(2,1)}, u32[]{:S(2)}) copy-start(bf16[1536,512]{1,0:T(8,128)(2,1)} %copy-done.5) | copy-start | bytes 4718596
  218.1 1.4 copy-start.3
  219.5 1.4 copy-start.4
  220.9 23.1 %copy-start.12 = (bf16[1536,512]{1,0:T(8,128)(2,1)S(1)}, bf16[1536,512]{1,0:T(8,128)(2,1)}, u32[]{:S(2)}) copy-start(bf16[1536,512]{1,0:T(8,128)(2,1)} %get-tuple-element.65) | copy-start | bytes 4718596
  244.1 4.8 %copy-start.1 = (f32[2048,512]{1,0:T(8,128)S(1)}, f32[2048,512]{1,0:T(8,128)}, u32[]{:S(2)}) copy-start(f32[2048,512]{1,0:T(8,128)} %get-tuple-element.64) | copy-start | bytes 12582916
  244.1 4.9 %copy-start.2 = (f32[512,2048]{1,0:T(8,128)S(1)}, f32[512,2048]{1,0:T(8,128)}, u32[]{:S(2)}) copy-start(f32[512,2048]{1,0:T(8,128)} %get-tuple-element.63) | copy-start | bytes 12582916
  244.1 5.1 %copy-start.8 = (f32[512,512]{1,0:T(8,128)S(1)}, f32[512,512]{1,0:T(8,128)}, u32[]{:S(2)}) copy-start(f32[512,512]{1,0:T(8,128)} %get-tuple-element.69) | copy-start | bytes 3145732
  249.2 47.2 %copy-start.11 = (bf16[1536,512]{1,0:T(8,128)(2,1)S(1)}, bf16[1536,512]{1,0:T(8,128)(2,1)}, u32[]{:S(2)}) copy-start(bf16[1536,512]{1,0:T(8,128)(2,1)} %get-tuple-element.78) | copy-start | bytes 4718596

commit v2 on v1

--- a/solution.py
+++ b/solution.py
@@ -105,11 +105,11 @@
 
 def attn_fwd(qkv, seq, scale):
     tokens, width = qkv.shape[0], qkv.shape[1] // 3
-    spec = lambda off: pl.BlockSpec((seq, width // 2), lambda b, j: (b, off + j))
+    spec = lambda off: pl.BlockSpec((seq, width), lambda b: (b, off))
     return pl.pallas_call(
         functools.partial(attn_fwd_kernel, scale),
-        grid=(tokens // seq, 2),
-        in_specs=[spec(0), spec(2), spec(4)],
+        grid=(tokens // seq,),
+        in_specs=[spec(0), spec(1), spec(2)],
         out_specs=spec(0),
         out_shape=jax.ShapeDtypeStruct((tokens, width), BF),
         name="attn_fwd",
@@ -153,17 +153,12 @@
     n2 = rms_norm(mid_f32).astype(BF)
     n2_ref[...] = n2
     ff = wu_ref.shape[1]
-
-    def chunk(c, _):
-        cols = pl.ds(pl.multiple_of(c * 512, 512), 512)
-        up = dot(n2_ref[...], wu_ref[:, cols]).astype(BF)
-        up_ref[:, cols] = up
+    for c in range(0, ff, 512):
+        up = dot(n2, wu_ref[:, c:c + 512]).astype(BF)
+        up_ref[:, c:c + 512] = up
         u = up.astype(F32)
         t = jnp.tanh(u * (GELU_A + GELU_B * (u * u)))
-        ge_ref[:, cols] = (u * (0.5 * t + 0.5)).astype(BF)
-        return 0
-
-    lax.fori_loop(0, ff // 512, chunk, 0)
+        ge_ref[:, c:c + 512] = (u * (0.5 * t + 0.5)).astype(BF)
     out_ref[...] = (mid_f32 + dot(ge_ref[...], wd_ref[...])).astype(BF)
 
 
@@ -609,15 +604,7 @@
         ctu[rows, :] = gelu_pull(up_ref[rows, :].astype(F32), cg).astype(BF)
     gd_ref[...] = dot_tn(ge_ref[...], ct_ref[...])
     gu_ref[...] = dot_tn(n2_ref[...], ctu[...])
-    part = dot_nt(ctu[...], wu_ref[...])
-
-    @pl.when(step == 0)
-    def _():
-        acc[...] = part
-
-    @pl.when(step > 0)
-    def _():
-        acc[...] += part
+    acc[...] = jnp.where(step == 0, 0.0, acc[...]) + dot_nt(ctu[...], wu_ref[...])
 
     @pl.when(step == last)
     def _():
@@ -664,12 +651,22 @@
     )(*(args if carry else (first,) + args))
 
 
-def attn_carry_kernel(scale, width, q_ref, k_ref, v_ref, do_ref, acc_hbm, dqkv_ref, *rest):
-    results, (acc_ref, sup, sdown, sqkv, sproj, t1b, t2b, t1c, t2c, load_sem, send_sem, recv_sem, fsend_sem, frecv_sem) = rest[:4], rest[4:]
+def attn_carry_kernel(scale, width, q_ref, k_ref, v_ref, do_ref, acc_hbm, h2_hbm, dqkv_ref, *rest):
+    results, act_hbm = rest[:4], rest[4]
+    acc_ref, sup, sdown, sqkv, sproj, t1b, t2b, t1c, t2c, load_sem, send_sem, recv_sem, fsend_sem, frecv_sem, act_sem = rest[5:]
     steps = pl.num_programs(1)
     step = pl.program_id(0) * steps + pl.program_id(1)
     red = Reducer(acc_ref, (None, (t1b, t2b), (t1c, t2c)), (send_sem, recv_sem), start=1)
     outs, sems = (sup, sdown, sqkv, sproj), (fsend_sem, frecv_sem)
+
+    def act_copies():
+        where = act_hbm.at[pl.ds(red.pp * h2_hbm.shape[0], h2_hbm.shape[0])]
+        keep = pltpu.make_async_copy(h2_hbm.at[:, red.pp], where, act_sem.at[0])
+        give = pltpu.make_async_remote_copy(
+            src_ref=h2_hbm.at[:, red.partner], dst_ref=where, send_sem=act_sem.at[1], recv_sem=act_sem.at[2],
+            device_id={"pp": red.partner}, device_id_type=MESH)
+        come = pltpu.make_async_copy(h2_hbm.at[:, red.pp], act_hbm.at[pl.ds(red.partner * h2_hbm.shape[0], h2_hbm.shape[0])], act_sem.at[2])
+        return keep, give, come
 
     def begin():
         load = pltpu.make_async_copy(acc_hbm, acc_ref, load_sem)
@@ -677,6 +674,9 @@
         enter(red.me, red.partner)
         load.wait()
         red.all_first(1)
+        keep, give, _ = act_copies()
+        keep.start()
+        give.start()
 
     def turn():
         red.fourth(1)
@@ -699,11 +699,15 @@
         end_finals(red, outs, sems)
         red.drain(1)
         red.drain(2)
+        keep, give, come = act_copies()
+        keep.wait()
+        give.wait_send()
+        come.wait()
         for result, out in zip(results, outs):
             result[...] = out[...]
 
 
-def attn_bwd(qkv, do, seq, scale, carried):
+def attn_bwd(qkv, do, seq, scale, carried, h2):
     tokens, width = qkv.shape[0], qkv.shape[1] // 3
     steps = width // 256
     spec = lambda off: pl.BlockSpec((seq, 256), lambda b, j: (b, off + j))
@@ -712,13 +716,14 @@
     out_shape = [jax.ShapeDtypeStruct((tokens, 3 * width), BF)]
     args, scratch, params, kernel = (qkv, qkv, qkv, do), [], {}, attn_bwd_kernel
     if carried is not None:
-        args = args + (carried,)
+        h2 = h2.reshape(tokens // seq, 2, seq // 2, width)
+        args = args + (carried, h2)
         kernel = attn_carry_kernel
-        in_specs = in_specs + [pl.BlockSpec(memory_space=pl.ANY)]
+        in_specs = in_specs + [pl.BlockSpec(memory_space=pl.ANY)] * 2
         shapes = ((8, 2048), (32, 512), (8, 1536), (8, 512))
-        out_specs = out_specs + [whole(s) for s in shapes]
-        out_shape = out_shape + [jax.ShapeDtypeStruct(s, F32) for s in shapes]
-        scratch = [VMEM(s, F32) for s in (carried.shape,) + shapes] + PHASE_SCRATCH[1] + PHASE_SCRATCH[2] + [DMA] + PHASE_SEMS(2) + FINAL_SEMS
+        out_specs = out_specs + [whole(s) for s in shapes] + [pl.BlockSpec(memory_space=pl.ANY)]
+        out_shape = out_shape + [jax.ShapeDtypeStruct(s, F32) for s in shapes] + [jax.ShapeDtypeStruct((2 * h2.shape[0],) + h2.shape[2:], BF)]
+        scratch = [VMEM(s, F32) for s in (carried.shape,) + shapes] + PHASE_SCRATCH[1] + PHASE_SCRATCH[2] + [DMA] + PHASE_SEMS(2) + FINAL_SEMS + [DMA((3,))]
         params = dict(collective_id=3, has_side_effects=True, vmem_limit_bytes=50 << 20)
     return pl.pallas_call(
         functools.partial(kernel, scale, width),
@@ -736,27 +741,25 @@
     return out, (hidden, normed, qkv, attn, mid, normed2, up, gelu)
 
 
-def layer_backward(saved, ct_out, first, weights, layer, seq, scale, carried):
+def layer_backward(saved, ct_out, first, weights, layer, seq, scale, carried, h2):
     w_qkv, w_proj, w_up, w_down = weights
     hidden, normed, qkv, attn, mid, normed2, up, gelu = saved
     res = ffn_bwd(gelu, up, ct_out, first, normed2, mid, attn, w_down, w_up, w_proj, layer, seq, carried)
     g_down, g_up, g_proj, ct_mid, ct_attn = res[:5]
-    res = attn_bwd(qkv, ct_attn, seq, scale, res[5] if carried is not None else None)
+    res = attn_bwd(qkv, ct_attn, seq, scale, res[5] if carried is not None else None, h2)
     ct_qkv = res[0]
     g_qkv = dot_tn(normed, ct_qkv)
     grads = (g_qkv, g_proj, g_up, g_down)
     if carried is not None:
-        return grads, (res[3], res[4], res[1], res[2])
+        return grads, (res[3], res[4], res[1], res[2]), res[5]
     ct_norm = dot_nt(ct_qkv, w_qkv[layer]).astype(BF)
     ct_hidden = (ct_mid.astype(F32) + rms_pull(hidden.astype(F32), ct_norm.astype(F32))).astype(BF)
     return grads, ct_hidden
 
 
 def solution(mesh):
-    stages = mesh.shape['pp']
     grid = Mesh(mesh.devices.reshape(2, 4, 4, 4), ("pp", "z", "y", "x"))
     dp = ("z", "y", "x")
-    swap = [(0, 1), (1, 0)]
 
     def device_step(act_in, loss_seed, w_qkv, w_proj, w_up, w_down):
         micro, _, seq, d = act_in.shape
@@ -772,15 +775,9 @@
         h1, saved0 = layer_forward(act, pp_vec * mine, tokens, full, 0, seq, scale)
         h2, saved1 = layer_forward(h1, none, tokens, full, 1, seq, scale)
 
-        out4 = h2.reshape(mine, 1, seq, d)
-        half = seq // 2
-        keep = lax.dynamic_slice_in_dim(out4, pp * half, half, 2)
-        give = lax.dynamic_slice_in_dim(out4, (1 - pp) * half, half, 2)
-        got = lax.ppermute(give, 'pp', swap)
-        act_out = jnp.concatenate([jnp.where(pp == 0, keep, got), jnp.where(pp == 0, got, keep)], axis=0)
-
-        grads1, ct1 = layer_backward(saved1, seed, pp_vec, full, 1, seq, scale, None)
-        grads0, red1 = layer_backward(saved0, ct1, None, full, 0, seq, scale, grads1)
+        grads1, ct1 = layer_backward(saved1, seed, pp_vec, full, 1, seq, scale, None, None)
+        grads0, red1, act_out = layer_backward(saved0, ct1, None, full, 0, seq, scale, grads1, h2)
+        act_out = act_out.reshape(micro, 1, seq // 2, d)
         red0 = reduce_grads(grads0, 0)
         outs = [jnp.where(pp == 0, a, b) for a, b in zip(red0, red1)]
         return tuple(o.reshape(w.shape) for o, w in zip(outs, (w_qkv, w_proj, w_up, w_down))) + (act_out,)

time: 300 us -> 282 us (0.940)
  Pallas kernels: 266 us -> 254 us
    pallas_call x2, Pallas kernels: 37.5 us -> 31.6 us  [post_attn(): pl.pallas_call(post_kernel, grid_spec=pltpu.PrefetchScalarGridSpec(num_sc...]
    pallas_call x2, Pallas kernels: 62.4 us -> 58.7 us  [ffn_bwd(): pl.pallas_call(functools.partial(ffn_bwd_kernel, tile, carry), grid_spec=...]
  transfers between devices with their start and end apart: 1 -> 0, of which waited for: 0 -> 0; matrix products, arithmetic and copies ran while one was open for 7% -> 0% of each run, Pallas kernels for 50% -> 0%
where the time goes in v2:
time: 282 us
  Pallas kernels  254 us (90%)
  matrix products  14.3 us (5%)
  local copies, waits for them, and re-layouts  8.8 us (3%)
  other arithmetic  3.89 us (1%)
    pallas_call x2, Pallas kernels, ffn_bwd(): pl.pallas_call(functools.partial(ffn_bwd_kernel, tile, carry), grid_spec=...  58.7 us
    pallas_call x1, Pallas kernels, gather_weights(): pl.pallas_call(gather_kernel, in_specs=[vmem] * 4, out_specs=[pl.BlockSpe...  45.6 us
    pallas_call x1, Pallas kernels, reduce_grads(): pl.pallas_call(reduce_kernel, in_specs=[pl.BlockSpec(memory_space=pl.ANY)...  44.6 us
    pallas_call x2, Pallas kernels, attn_bwd(): pl.pallas_call(functools.partial(kernel, scale, width), grid=(tokens // s...  42.4 us
    pallas_call x2, Pallas kernels, post_attn(): pl.pallas_call(post_kernel, grid_spec=pltpu.PrefetchScalarGridSpec(num_sc...  31.6 us
    pallas_call x2, Pallas kernels, attn_fwd(): pl.pallas_call(functools.partial(attn_fwd_kernel, scale), grid=(tokens //...  17.5 us
    pallas_call x2, Pallas kernels, pre_attn(): pl.pallas_call(pre_kernel, grid_spec=pltpu.PrefetchScalarGridSpec(num_sca...  13.3 us
    dot_general x2, matrix products, dot_tn(): lax.dot_general(a, b, (((0,), (0,)), ((), ())), preferred_element_type=F32)  9.03 us

profile of v2, /device:TPU:1, one launch (start us, length us, event | category | flops | bytes accessed | tf_op | source)
XLA Modules:
  0.0 281.5 jit_solution(15240878634359448638)
XLA Ops:
  0.6 1.5 reshape.107.qkv_ref
  2.2 45.6 %gather_weights.1 = (bf16[2,4,4,4,8,2048]{5,4,3,2,1,0:T(8,128)(2,1)}, bf16[2,4,4,4,32,512]{5,4,3,2,1,0:T(8,128)(2,1)}, bf16[2,4,4,4,8,1536]{5,4,3,2,1,0:T(8,128)(2,1)}, bf16[2,4,4,4,8,512]{5,4,3,2,1,0:T(8,128)(2,1)}) custom-call(bf16[8,2048]{1,0:T(8,128)(2,1)} %bitcast.65, bf16[32,512]{1,0:T(8,128)(2,1)} %bitcast.66, bf16[8,1536]{1,0:T(8,128)(2,1)} %reshape.107.qkv_ref, ...), custom_call_target="tpu_custom_call" | custom-call | tf_op jit(solution)/shard_map/gather_weights/pallas_call | solution.py:308
  47.8 1.5 slice.4
  49.3 6.7 %pre_attn.2 = (bf16[1536,512]{1,0:T(8,128)(2,1)}, bf16[1536,1536]{1,0:T(8,128)(2,1)}) custom-call(s32[1]{0:T(128)S(6)} %mul.49._, bf16[3072,512]{1,0:T(8,128)(2,1)} %bitcast.57, bf16[2,512,1536]{2,1,0:T(8,128)(2,1)} %bitcast.55), custom_call_target="tpu_custom_call" | custom-call | tf_op jit(solution)/shard_map/pre_attn/pallas_call | solution.py:138
  56.0 8.7 %attn_fwd.2.a_ref.refs_5_ = bf16[1536,512]{1,0:T(8,128)(2,1)} custom-call(bf16[1536,1536]{1,0:T(8,128)(2,1)} %get-tuple-element.44.q_ref.k_ref.v_ref, bf16[1536,1536]{1,0:T(8,128)(2,1)} %get-tuple-element.44.q_ref.k_ref.v_ref, bf16[1536,1536]{1,0:T(8,128)(2,1)} %get-tuple-element.44.q_ref.k_ref.v_ref), custom_call_target="tpu_custom_call" | custom-call | tf_op jit(solution)/shard_map/attn_fwd/pallas_call | solution.py:109
  64.8 15.8 %post_attn.2 = (bf16[1536,512]{1,0:T(8,128)(2,1)}, bf16[1536,512]{1,0:T(8,128)(2,1)}, bf16[1536,2048]{1,0:T(8,128)(2,1)}, bf16[1536,2048]{1,0:T(8,128)(2,1)}, bf16[1536,512]{1,0:T(8,128)(2,1)}) custom-call(s32[1]{0:T(128)S(6)} %mul.49._, bf16[3072,512]{1,0:T(8,128)(2,1)} %bitcast.58, bf16[1536,512]{1,0:T(8,128)(2,1)} %attn_fwd.2.a_ref.refs_5_, ...), custom_call_target="tpu_custom_call" | custom-call | tf_op jit(solution)/shard_map/post_attn/pallas_call | solution.py:169
  80.5 6.6 %pre_attn.3 = (bf16[1536,512]{1,0:T(8,128)(2,1)}, bf16[1536,1536]{1,0:T(8,128)(2,1)}) custom-call(s32[1]{0:T(128)} %constant.16.clone.1._, bf16[1536,512]{1,0:T(8,128)(2,1)} %get-tuple-element.50.h_ref, bf16[2,512,1536]{2,1,0:T(8,128)(2,1)} %bitcast.56), custom_call_target="tpu_custom_call" | custom-call | tf_op jit(solution)/shard_map/pre_attn/pallas_call | solution.py:138
  87.1 8.7 %attn_fwd.3.a_ref.refs_6_ = bf16[1536,512]{1,0:T(8,128)(2,1)} custom-call(bf16[1536,1536]{1,0:T(8,128)(2,1)} %get-tuple-element.51.q_ref.k_ref.v_ref, bf16[1536,1536]{1,0:T(8,128)(2,1)} %get-tuple-element.51.q_ref.k_ref.v_ref, bf16[1536,1536]{1,0:T(8,128)(2,1)} %get-tuple-element.51.q_ref.k_ref.v_ref), custom_call_target="tpu_custom_call" | custom-call | tf_op jit(solution)/shard_map/attn_fwd/pallas_call | solution.py:109
  95.9 15.8 %post_attn.3 = (bf16[1536,512]{1,0:T(8,128)(2,1)}, bf16[1536,512]{1,0:T(8,128)(2,1)}, bf16[1536,2048]{1,0:T(8,128)(2,1)}, bf16[1536,2048]{1,0:T(8,128)(2,1)}, bf16[1536,512]{1,0:T(8,128)(2,1)}) custom-call(s32[1]{0:T(128)} %constant.16.clone.1._, bf16[1536,512]{1,0:T(8,128)(2,1)} %get-tuple-element.50.h_ref, bf16[1536,512]{1,0:T(8,128)(2,1)} %attn_fwd.3.a_ref.refs_6_, ...), custom_call_target="tpu_custom_call" | custom-call | tf_op jit(solution)/shard_map/post_attn/pallas_call | solution.py:169
  111.7 0.0 copy-done
  111.7 24.2 %ffn_bwd.1 = (f32[2048,512]{1,0:T(8,128)}, f32[512,2048]{1,0:T(8,128)}, f32[512,512]{1,0:T(8,128)S(1)}, bf16[1536,512]{1,0:T(8,128)(2,1)S(1)}, bf16[1536,512]{1,0:T(8,128)(2,1)}) custom-call(s32[1]{0:T(128)} %bitcast.refs_0_, bf16[1536,2048]{1,0:T(8,128)(2,1)} %get-tuple-element.52.refs_1_, bf16[1536,2048]{1,0:T(8,128)(2,1)} %get-tuple-element.53.refs_2_, ...), custom_call_target="tpu_custom_call" | custom-call | tf_op jit(solution)/shard_map/ffn_bwd/pallas_call | solution.py:644
  135.9 0.0 copy-start.4
  135.9 1.1 copy-done.4
  137.0 1.0 copy-done.6
  138.0 19.2 %attn_bwd.1 = bf16[1536,1536]{1,0:T(8,128)(2,1)} custom-call(bf16[1536,1536]{1,0:T(8,128)(2,1)} %get-tuple-element.51.q_ref.k_ref.v_ref, bf16[1536,1536]{1,0:T(8,128)(2,1)} %get-tuple-element.51.q_ref.k_ref.v_ref, bf16[1536,1536]{1,0:T(8,128)(2,1)} %get-tuple-element.51.q_ref.k_ref.v_ref, bf16[1536,512]{1,0:T(8,128)(2,1)} %get-tuple-element.57.do_ref), custom_call_target="tpu_custom_call" | custom-call | tf_op jit(solution)/shard_map/attn_bwd/pallas_call | solution.py:728
  157.2 0.0 copy-done.8
  157.2 5.3 %fusion.3 = (f32[1536]{0:T(1024)S(1)}, f32[1536]{0:T(1024)S(1)}, bf16[1536,512]{1,0:T(8,128)(2,1)S(1)}) fusion(bf16[1536,512]{1,0:T(8,128)(2,1)S(1)} %copy-done.8, bf16[1536,1536]{1,0:T(8,128)(2,1)} %attn_bwd.1, bf16[512,1536]{1,0:T(8,128)(2,1)S(1)} %bitcast.64), kind=kOutput, calls=%fused_computation.7 | convolution fusion | flops 2421421056 | bytes 9449472 | tf_op jit(solution)/shard_map/dot_general | solution.py:25
  162.6 4.3 %fusion.6 = f32[512,1536]{1,0:T(8,128)} fusion(bf16[1536,512]{1,0:T(8,128)(2,1)S(1)} %copy-done.11, bf16[1536,1536]{1,0:T(8,128)(2,1)S(1)} %copy-done.9), kind=kOutput, calls=%fused_computation.17 | convolution fusion | flops 2415919104 | bytes 9437184 | tf_op jit(solution)/shard_map/dot_general | solution.py:29
  166.9 2.0 fusion.2.refs_2_
  168.9 34.5 %ffn_bwd_carry.1 = (f32[2048,512]{1,0:T(8,128)}, f32[512,2048]{1,0:T(8,128)}, f32[512,512]{1,0:T(8,128)}, bf16[1536,512]{1,0:T(8,128)(2,1)}, bf16[1536,512]{1,0:...) custom-call(bf16[1536,2048]{1,0:T(8,128)(2,1)} %get-tuple-element.48.refs_0_, bf16[1536,2048]{1,0:T(8,128)(2,1)} %get-tuple-element.49.refs_1_, ...), custom_call_target="tpu_custom_call" | custom-call | tf_op jit(solution)/shard_map/ffn_bwd_carry/pallas_call | solution.py:644
  203.4 1.4 copy-done.3
  204.8 23.2 %attn_bwd_carry.1 = (bf16[1536,1536]{1,0:T(8,128)(2,1)}, f32[8,2048]{1,0:T(8,128)S(1)}, f32[32,512]{1,0:T(8,128)S(1)}, f32[8,1536]{1,0:T(8,128)S(1)}, f32[8,512]...) custom-call(bf16[1536,1536]{1,0:T(8,128)(2,1)} %get-tuple-element.44.q_ref.k_ref.v_ref, ...), custom_call_target="tpu_custom_call" | custom-call | tf_op jit(solution)/shard_map/attn_bwd_carry/pallas_call | solution.py:728
  228.1 4.7 %fusion.7 = f32[512,1536]{1,0:T(8,128)S(1)} fusion(bf16[1536,512]{1,0:T(8,128)(2,1)S(1)} %copy-done.10, bf16[1536,1536]{1,0:T(8,128)(2,1)} %get-tuple-element.70), kind=kOutput, calls=%fused_computation.18 | convolution fusion | flops 2415919104 | bytes 9437184 | tf_op jit(solution)/shard_map/dot_general | solution.py:29
  232.8 0.0 copy-done.1
  232.9 0.1 copy-done.2
  233.0 0.2 copy-done.7
  233.2 44.6 %reduce_grads.1 = (f32[8,2048]{1,0:T(8,128)S(1)}, f32[32,512]{1,0:T(8,128)S(1)}, f32[8,1536]{1,0:T(8,128)S(1)}, f32[8,512]{1,0:T(8,128)S(1)}) custom-call(f32[4,4,4,8,2048]{4,3,2,1,0:T(8,128)S(1)} %bitcast.42, f32[4,4,4,32,512]{4,3,2,1,0:T(8,128)S(1)} %bitcast.41, f32[4,4,4,8,1536]{4,3,2,1,0:T(8,128)S(1)} %bitcast.43, f32[4,4,4,8,512]{4,3,2,1,0:T(8,128)S(1)} %bitcast.46), custom_call_target="tpu_custom_call" | custom-call | tf_op jit(solution)/shard_map/reduce_grads/pallas_call | solution.py:535
  277.8 0.6 select_bitcast_fusion
  278.4 0.6 select_bitcast_fusion.1
  279.1 0.6 select_bitcast_fusion.2
  279.7 0.7 reshape.123
  280.4 1.1 copy.15
  (17 shorter events, 0.0 us)
Async XLA Ops:
  95.8 15.8 %copy-start = (bf16[2,4,4,4,8,512]{5,4,3,2,1,0:T(8,128)(2,1)S(1)}, bf16[2,4,4,4,8,512]{5,4,3,2,1,0:T(8,128)(2,1)}, u32[]{:S(2)}) copy-start(bf16[2,4,4,4,8,512]{5,4,3,2,1,0:T(8,128)(2,1)} %get-tuple-element.45) | copy-start | bytes 3145732
  135.9 1.2 copy-start.4
  137.0 1.0 copy-start.6
  138.0 19.2 %copy-start.8 = (bf16[1536,512]{1,0:T(8,128)(2,1)S(1)}, bf16[1536,512]{1,0:T(8,128)(2,1)}, u32[]{:S(2)}) copy-start(bf16[1536,512]{1,0:T(8,128)(2,1)} %get-tuple-element.50.h_ref) | copy-start | bytes 4718596
  157.2 5.3 %copy-start.9 = (bf16[1536,1536]{1,0:T(8,128)(2,1)S(1)}, bf16[1536,1536]{1,0:T(8,128)(2,1)}, u32[]{:S(2)}) copy-start(bf16[1536,1536]{1,0:T(8,128)(2,1)} %attn_bwd.1) | copy-start | bytes 14155780
  157.2 5.3 %copy-start.11 = (bf16[1536,512]{1,0:T(8,128)(2,1)S(1)}, bf16[1536,512]{1,0:T(8,128)(2,1)}, u32[]{:S(2)}) copy-start(bf16[1536,512]{1,0:T(8,128)(2,1)} %get-tuple-element.62) | copy-start | bytes 4718596
  162.6 4.3 %copy-start.5 = (bf16[1536,512]{1,0:T(8,128)(2,1)S(1)}, bf16[1536,512]{1,0:T(8,128)(2,1)}, u32[]{:S(2)}) copy-start(bf16[1536,512]{1,0:T(8,128)(2,1)} %copy-done.4) | copy-start | bytes 4718596
  203.4 1.4 copy-start.3
  204.8 23.3 %copy-start.10 = (bf16[1536,512]{1,0:T(8,128)(2,1)S(1)}, bf16[1536,512]{1,0:T(8,128)(2,1)}, u32[]{:S(2)}) copy-start(bf16[1536,512]{1,0:T(8,128)(2,1)} %get-tuple-element.66) | copy-start | bytes 4718596
  228.1 4.8 %copy-start.1 = (f32[2048,512]{1,0:T(8,128)S(1)}, f32[2048,512]{1,0:T(8,128)}, u32[]{:S(2)}) copy-start(f32[2048,512]{1,0:T(8,128)} %get-tuple-element.65) | copy-start | bytes 12582916
  228.1 4.9 %copy-start.2 = (f32[512,2048]{1,0:T(8,128)S(1)}, f32[512,2048]{1,0:T(8,128)}, u32[]{:S(2)}) copy-start(f32[512,2048]{1,0:T(8,128)} %get-tuple-element.64) | copy-start | bytes 12582916
  228.1 5.1 %copy-start.7 = (f32[512,512]{1,0:T(8,128)S(1)}, f32[512,512]{1,0:T(8,128)}, u32[]{:S(2)}) copy-start(f32[512,512]{1,0:T(8,128)} %get-tuple-element.71) | copy-start | bytes 3145732
